TPU v7x, 128 devices: a whole 4x4x4 slice. The times are simulated.
128 devices in a mesh: dp: 1, tp: 16 (over z, y), cp: 8 (over x, core).
Axes of the slice: x: 4, y: 4, z: 4, core: 2. Of those that a mesh axis runs over, the one named last changes fastest.
Arguments:
- x: bfloat16 [16384, 4608], P(('dp', 'cp', 'tp'))
- w_q: bfloat16 [4608, 4096], P(None, 'tp')
- w_k: bfloat16 [4608, 2048], P(None, 'tp')
- w_v: bfloat16 [4608, 2048], P(None, 'tp')
- w_o: bfloat16 [4096, 4608], P('tp')
Outputs:
- output: bfloat16 [16384, 4608], P(('dp', 'cp', 'tp'))
All inputs are finite; a program needn't handle non-finite values.
Results may differ from a plain program's by a relative error of at most 0.00601587.
Values are sent between devices in bfloat16 or wider.
A program may use at most 1 GiB of HBM per device.

v0:
```python
import jax
import jax.numpy as jnp
from jax import lax
from jax.sharding import PartitionSpec as P

HEAD_DIM = 128


def block_scores(q_part, k_part):
    raw_scores = jnp.einsum("qhge,khe->hgqk", q_part, k_part, preferred_element_type=jnp.float32)
    return raw_scores * (HEAD_DIM ** -0.5)


def merge_block(soft_state, scores, v_part):
    run_max, run_sum, run_acc = soft_state
    new_max = jnp.maximum(run_max, scores.max(axis=-1))
    rescale = jnp.exp(run_max - new_max)
    p_block = jnp.exp(scores - new_max[..., None])
    new_sum = run_sum * rescale + p_block.sum(axis=-1)
    new_acc = run_acc * rescale[..., None] + jnp.einsum("hgqk,khe->hgqe", p_block.astype(jnp.bfloat16), v_part, preferred_element_type=jnp.float32)
    return new_max, new_sum, new_acc


def solution(mesh):
    cp_size = mesh.shape["cp"]
    row_spec = P(("dp", "cp", "tp"), None)

    def local_layer(x_loc, w_q, w_k, w_v, w_o):
        model_width = x_loc.shape[1]
        kv_local = w_k.shape[1] // HEAD_DIM
        group_size = w_q.shape[1] // w_k.shape[1]
        x_block = lax.all_gather(x_loc, "tp", axis=0, tiled=True)
        piece_len = x_block.shape[0] // 2
        q_all = jnp.dot(x_block, w_q, preferred_element_type=jnp.float32).astype(jnp.bfloat16).reshape(2, piece_len, kv_local, group_size, HEAD_DIM)
        k_all = jnp.dot(x_block, w_k, preferred_element_type=jnp.float32).astype(jnp.bfloat16).reshape(2, piece_len, kv_local, HEAD_DIM)
        v_all = jnp.dot(x_block, w_v, preferred_element_type=jnp.float32).astype(jnp.bfloat16).reshape(2, piece_len, kv_local, HEAD_DIM)
        q_low = q_all[0]
        q_high = q_all[1]
        cp_rank = lax.axis_index("cp")
        offsets = jnp.arange(piece_len)
        pos_low = cp_rank * piece_len + offsets
        pos_high = (2 * cp_size - 1 - cp_rank) * piece_len + offsets
        pos_both = jnp.concatenate([pos_low, pos_high])
        stat_shape = (kv_local, group_size, piece_len)
        empty_state = (jnp.full(stat_shape, -jnp.inf, jnp.float32), jnp.zeros(stat_shape, jnp.float32), jnp.zeros(stat_shape + (HEAD_DIM,), jnp.float32))
        k_flat = k_all.reshape(2 * piece_len, kv_local, HEAD_DIM)
        v_flat = v_all.reshape(2 * piece_len, kv_local, HEAD_DIM)
        low_scores = jnp.where(pos_low[:, None] >= pos_low[None, :], block_scores(q_low, k_all[0]), -jnp.inf)
        high_scores = jnp.where(pos_high[:, None] >= pos_both[None, :], block_scores(q_high, k_flat), -jnp.inf)
        own_states = (merge_block(empty_state, low_scores, v_all[0]), merge_block(empty_state, high_scores, v_flat))

        def earlier_source(states, kv_src):
            state_low, state_high = states
            k_src = kv_src[0, 0]
            v_src = kv_src[1, 0]
            return (merge_block(state_low, block_scores(q_low, k_src), v_src), merge_block(state_high, block_scores(q_high, k_src), v_src))

        def later_source(states, kv_src):
            state_low, state_high = states
            k_src = kv_src[0].reshape(2 * piece_len, kv_local, HEAD_DIM)
            v_src = kv_src[1].reshape(2 * piece_len, kv_local, HEAD_DIM)
            return (state_low, merge_block(state_high, block_scores(q_high, k_src), v_src))

        shift_pairs = [(dev_idx, (dev_idx + 1) % cp_size) for dev_idx in range(cp_size)]

        def kv_step(step_idx, loop_carry):
            states, kv_held = loop_carry
            kv_held = lax.ppermute(kv_held, "cp", shift_pairs)
            source = (cp_rank - step_idx) % cp_size
            states = lax.cond(source < cp_rank, earlier_source, later_source, states, kv_held)
            return states, kv_held

        kv_pair = jnp.stack([k_all, v_all])
        final_carry = lax.fori_loop(1, cp_size, kv_step, (own_states, kv_pair))
        state_low, state_high = final_carry[0]
        out_low = (state_low[2] / state_low[1][..., None]).astype(jnp.bfloat16)
        out_high = (state_high[2] / state_high[1][..., None]).astype(jnp.bfloat16)
        attn_out = jnp.stack([out_low, out_high], axis=2)
        w_o_heads = w_o.reshape(kv_local, group_size, HEAD_DIM, model_width)
        partial = jnp.einsum("hgsqe,hged->sqd", attn_out, w_o_heads, preferred_element_type=jnp.float32).reshape(2 * piece_len, model_width)
        y_loc = lax.psum_scatter(partial, "tp", scatter_dimension=0, tiled=True)
        return y_loc.astype(jnp.bfloat16)

    return jax.shard_map(local_layer, mesh=mesh, in_specs=(row_spec, P(None, "tp"), P(None, "tp"), P(None, "tp"), P("tp", None)), out_specs=row_spec, check_vma=False)
```

profile of v0, /device:TPU:0, one launch (start us, length us, event | category | flops | bytes accessed | tf_op | source)
XLA Modules:
  0.0 757.4 jit_solution(3267287645252680341)
XLA Ops:
  10.3 123.7 %all-gather.2.cloned.1.call-done = bf16[2048,4608]{1,0:T(8,128)(2,1)} async-done(((bf16[128,4608]{1,0:T(8,128)(2,1)}), bf16[2048,4608]{1,0:T(8,128)(2,1)}) %all-gather.2.cloned.1.call-update) | async-done | bytes 18874384 | tf_op jit(solution)/shard_map/all_gather | solution.py:32
  134.0 9.7 %convolution_convert_fusion = bf16[2048,256]{0,1:T(8,128)(2,1)S(1)} fusion(bf16[2048,4608]{1,0:T(8,128)(2,1)} %all-gather.2.cloned.1.call-done, bf16[4608,256]{1,0:T(8,128)(2,1)} %param.10), kind=kOutput, calls=%fused_computation.78 | convolution fusion | flops 4832362496 | bytes 22282240 | tf_op jit(solution)/shard_map/dot_general | solution.py:34
  148.9 9.4 %convolution_convert_fusion.2 = bf16[2048,128]{1,0:T(8,128)(2,1)S(1)} fusion(bf16[2048,4608]{1,0:T(8,128)(2,1)} %all-gather.2.cloned.1.call-done, bf16[4608,128]{1,0:T(8,128)(2,1)} %param.11), kind=kOutput, calls=%fused_computation.80 | convolution fusion | flops 2416181248 | bytes 20578304 | tf_op jit(solution)/shard_map/dot_general | solution.py:35
  170.9 24.6 %convolution_convert_fusion.1 = bf16[2048,128]{1,0:T(8,128)(2,1)S(1)} fusion(bf16[2048,4608]{1,0:T(8,128)(2,1)} %all-gather.2.cloned.1.call-done, bf16[4608,128]{1,0:T(8,128)(2,1)S(1)} %copy-done.12), kind=kOutput, calls=%fused_computation.79 | convolution fusion | flops 2416181248 | bytes 20578304 | tf_op jit(solution)/shard_map/dot_general | solution.py:36
  209.3 307.1 %while.27 = (s32[]{:T(128)}, f32[1,2,1024]{2,1,0:T(2,128)S(1)}, f32[1,2,1024]{2,1,0:T(2,128)S(1)}, f32[1,2,1024,128]{3,2,1,0:T(8,128)}, f32[1,2,1024]{2,1,0:T(2,...) while((s32[]{:T(128)}, f32[1,2,1024]{2,1,0:T(2,128)S(1)}, ...), condition=%wide.region_13.14_spmd, body=%wide.region_4.13_spmd.sunk | while | flops 2182098944 | bytes 82051704 | solution.py:74
  209.3 15.4 %collective-permute-done = bf16[2,2,1024,1,128]{4,2,3,1,0:T(8,128)(2,1)S(1)} collective-permute-done((bf16[2,2,1024,1,128]{4,2,3,1,0:T(8,128)(2,1)}, bf16[2,2,1024,1,128]{4,2,3,1,0:T(8,128)(2,1)S(1)}, u32[]{:S(2)}, u32[]{:S(2)}) %collective-permute-start) | collective-permute-done | bytes 1048608 | tf_op jit(solution)/shard_map/while/body/eval_jaxpr/ppermute | solution.py:68
  224.8 26.8 %conditional.2 = (f32[1,2,1024]{2,1,0:T(2,128)S(1)}, f32[1,2,1024]{2,1,0:T(2,128)S(1)}, f32[1,2,1024,128]{3,2,1,0:T(8,128)}, f32[1,2,1024]{2,1,0:T(2,128)}, f32[...) conditional(s32[]{:T(128)} %convert_element_type.101, (bf16[2,2,1024,1,128]{4,2,3,1,0:T(8,128)(2,1)S(1)}, ...), branch_computations={%region_5.7_spmd, %region_8.12_spmd} | conditional | flops 2182098944 | bytes 75743416 | solution.py:70
  224.8 9.1 %bitcast_reduce_fusion = (f32[2,1024]{1,0:T(2,128)S(1)}, f32[2048,1024,2]{1,0,2:T(8,128)}) fusion(bf16[2048,128,1]{1,0,2:T(8,128)(2,1)S(1)} %bitcast.266, bf16[1024,1,2,128]{3,0,2,1:T(8,128)(2,1)} %get-tuple-element.326), kind=kOutput, calls=%fused_computation.1 | convolution fusion | flops 1082128384 | bytes 17833984 | tf_op jit(solution)/shard_map/while/body/eval_jaxpr/cond/branch_0_fun/qhge,khe->hgqk/dot_general | solution.py:10
  253.2 15.4 %collective-permute-done = bf16[2,2,1024,1,128]{4,2,3,1,0:T(8,128)(2,1)S(1)} collective-permute-done((bf16[2,2,1024,1,128]{4,2,3,1,0:T(8,128)(2,1)}, bf16[2,2,1024,1,128]{4,2,3,1,0:T(8,128)(2,1)S(1)}, u32[]{:S(2)}, u32[]{:S(2)}) %collective-permute-start) | collective-permute-done | bytes 1048608 | tf_op jit(solution)/shard_map/while/body/eval_jaxpr/ppermute | solution.py:68
  268.6 26.8 %conditional.2 = (f32[1,2,1024]{2,1,0:T(2,128)S(1)}, f32[1,2,1024]{2,1,0:T(2,128)S(1)}, f32[1,2,1024,128]{3,2,1,0:T(8,128)}, f32[1,2,1024]{2,1,0:T(2,128)}, f32[...) conditional(s32[]{:T(128)} %convert_element_type.101, (bf16[2,2,1024,1,128]{4,2,3,1,0:T(8,128)(2,1)S(1)}, ...), branch_computations={%region_5.7_spmd, %region_8.12_spmd} | conditional | flops 2182098944 | bytes 75743416 | solution.py:70
  297.1 15.4 %collective-permute-done = bf16[2,2,1024,1,128]{4,2,3,1,0:T(8,128)(2,1)S(1)} collective-permute-done((bf16[2,2,1024,1,128]{4,2,3,1,0:T(8,128)(2,1)}, bf16[2,2,1024,1,128]{4,2,3,1,0:T(8,128)(2,1)S(1)}, u32[]{:S(2)}, u32[]{:S(2)}) %collective-permute-start) | collective-permute-done | bytes 1048608 | tf_op jit(solution)/shard_map/while/body/eval_jaxpr/ppermute | solution.py:68
  312.5 26.8 %conditional.2 = (f32[1,2,1024]{2,1,0:T(2,128)S(1)}, f32[1,2,1024]{2,1,0:T(2,128)S(1)}, f32[1,2,1024,128]{3,2,1,0:T(8,128)}, f32[1,2,1024]{2,1,0:T(2,128)}, f32[...) conditional(s32[]{:T(128)} %convert_element_type.101, (bf16[2,2,1024,1,128]{4,2,3,1,0:T(8,128)(2,1)S(1)}, ...), branch_computations={%region_5.7_spmd, %region_8.12_spmd} | conditional | flops 2182098944 | bytes 75743416 | solution.py:70
  312.6 9.1 %bitcast_reduce_fusion = (f32[2,1024]{1,0:T(2,128)S(1)}, f32[2048,1024,2]{1,0,2:T(8,128)}) fusion(bf16[2048,128,1]{1,0,2:T(8,128)(2,1)S(1)} %bitcast.266, bf16[1024,1,2,128]{3,0,2,1:T(8,128)(2,1)} %get-tuple-element.326), kind=kOutput, calls=%fused_computation.1 | convolution fusion | flops 1082128384 | bytes 17833984 | tf_op jit(solution)/shard_map/while/body/eval_jaxpr/cond/branch_0_fun/qhge,khe->hgqk/dot_general | solution.py:10
  341.0 15.4 %collective-permute-done = bf16[2,2,1024,1,128]{4,2,3,1,0:T(8,128)(2,1)S(1)} collective-permute-done((bf16[2,2,1024,1,128]{4,2,3,1,0:T(8,128)(2,1)}, bf16[2,2,1024,1,128]{4,2,3,1,0:T(8,128)(2,1)S(1)}, u32[]{:S(2)}, u32[]{:S(2)}) %collective-permute-start) | collective-permute-done | bytes 1048608 | tf_op jit(solution)/shard_map/while/body/eval_jaxpr/ppermute | solution.py:68
  356.4 26.8 %conditional.2 = (f32[1,2,1024]{2,1,0:T(2,128)S(1)}, f32[1,2,1024]{2,1,0:T(2,128)S(1)}, f32[1,2,1024,128]{3,2,1,0:T(8,128)}, f32[1,2,1024]{2,1,0:T(2,128)}, f32[...) conditional(s32[]{:T(128)} %convert_element_type.101, (bf16[2,2,1024,1,128]{4,2,3,1,0:T(8,128)(2,1)S(1)}, ...), branch_computations={%region_5.7_spmd, %region_8.12_spmd} | conditional | flops 2182098944 | bytes 75743416 | solution.py:70
  384.8 15.4 %collective-permute-done = bf16[2,2,1024,1,128]{4,2,3,1,0:T(8,128)(2,1)S(1)} collective-permute-done((bf16[2,2,1024,1,128]{4,2,3,1,0:T(8,128)(2,1)}, bf16[2,2,1024,1,128]{4,2,3,1,0:T(8,128)(2,1)S(1)}, u32[]{:S(2)}, u32[]{:S(2)}) %collective-permute-start) | collective-permute-done | bytes 1048608 | tf_op jit(solution)/shard_map/while/body/eval_jaxpr/ppermute | solution.py:68
  400.3 26.8 %conditional.2 = (f32[1,2,1024]{2,1,0:T(2,128)S(1)}, f32[1,2,1024]{2,1,0:T(2,128)S(1)}, f32[1,2,1024,128]{3,2,1,0:T(8,128)}, f32[1,2,1024]{2,1,0:T(2,128)}, f32[...) conditional(s32[]{:T(128)} %convert_element_type.101, (bf16[2,2,1024,1,128]{4,2,3,1,0:T(8,128)(2,1)S(1)}, ...), branch_computations={%region_5.7_spmd, %region_8.12_spmd} | conditional | flops 2182098944 | bytes 75743416 | solution.py:70
  400.3 9.1 %bitcast_reduce_fusion = (f32[2,1024]{1,0:T(2,128)S(1)}, f32[2048,1024,2]{1,0,2:T(8,128)}) fusion(bf16[2048,128,1]{1,0,2:T(8,128)(2,1)S(1)} %bitcast.266, bf16[1024,1,2,128]{3,0,2,1:T(8,128)(2,1)} %get-tuple-element.326), kind=kOutput, calls=%fused_computation.1 | convolution fusion | flops 1082128384 | bytes 17833984 | tf_op jit(solution)/shard_map/while/body/eval_jaxpr/cond/branch_0_fun/qhge,khe->hgqk/dot_general | solution.py:10
  428.7 15.4 %collective-permute-done = bf16[2,2,1024,1,128]{4,2,3,1,0:T(8,128)(2,1)S(1)} collective-permute-done((bf16[2,2,1024,1,128]{4,2,3,1,0:T(8,128)(2,1)}, bf16[2,2,1024,1,128]{4,2,3,1,0:T(8,128)(2,1)S(1)}, u32[]{:S(2)}, u32[]{:S(2)}) %collective-permute-start) | collective-permute-done | bytes 1048608 | tf_op jit(solution)/shard_map/while/body/eval_jaxpr/ppermute | solution.py:68
  444.1 26.8 %conditional.2 = (f32[1,2,1024]{2,1,0:T(2,128)S(1)}, f32[1,2,1024]{2,1,0:T(2,128)S(1)}, f32[1,2,1024,128]{3,2,1,0:T(8,128)}, f32[1,2,1024]{2,1,0:T(2,128)}, f32[...) conditional(s32[]{:T(128)} %convert_element_type.101, (bf16[2,2,1024,1,128]{4,2,3,1,0:T(8,128)(2,1)S(1)}, ...), branch_computations={%region_5.7_spmd, %region_8.12_spmd} | conditional | flops 2182098944 | bytes 75743416 | solution.py:70
  472.6 15.4 %collective-permute-done = bf16[2,2,1024,1,128]{4,2,3,1,0:T(8,128)(2,1)S(1)} collective-permute-done((bf16[2,2,1024,1,128]{4,2,3,1,0:T(8,128)(2,1)}, bf16[2,2,1024,1,128]{4,2,3,1,0:T(8,128)(2,1)S(1)}, u32[]{:S(2)}, u32[]{:S(2)}) %collective-permute-start) | collective-permute-done | bytes 1048608 | tf_op jit(solution)/shard_map/while/body/eval_jaxpr/ppermute | solution.py:68
  488.0 26.8 %conditional.2 = (f32[1,2,1024]{2,1,0:T(2,128)S(1)}, f32[1,2,1024]{2,1,0:T(2,128)S(1)}, f32[1,2,1024,128]{3,2,1,0:T(8,128)}, f32[1,2,1024]{2,1,0:T(2,128)}, f32[...) conditional(s32[]{:T(128)} %convert_element_type.101, (bf16[2,2,1024,1,128]{4,2,3,1,0:T(8,128)(2,1)S(1)}, ...), branch_computations={%region_5.7_spmd, %region_8.12_spmd} | conditional | flops 2182098944 | bytes 75743416 | solution.py:70
  519.8 14.2 %convolution_bitcast_fusion = f32[2048,4608]{1,0:T(8,128)} fusion(bf16[2048,128,2]{1,0,2:T(8,128)(2,1)S(1)} %bitcast.269, bf16[2,128,4608]{2,1,0:T(8,128)(2,1)S(1)} %bitcast.263), kind=kOutput, calls=%fused_computation.60 | convolution fusion | flops 4831838208 | bytes 41156608 | tf_op jit(solution)/shard_map/hgsqe,hged->sqd/dot_general | solution.py:80
  534.0 213.4 %reduce-scatter.2.cloned.1.call-done = f32[128,4608]{1,0:T(8,128)} async-done(((f32[2048,4608]{1,0:T(8,128)}), f32[128,4608]{1,0:T(8,128)}) %reduce-scatter.2.cloned.1.call-update) | async-done | bytes 2359312 | tf_op jit(solution)/shard_map/reduce_scatter | solution.py:81
  (127 shorter events, 212.8 us)
Async XLA Ops:
  6.5 513.3 %copy-start = (bf16[256,4608]{1,0:T(8,128)(2,1)S(1)}, bf16[256,4608]{1,0:T(8,128)(2,1)}, u32[]{:S(2)}) copy-start(bf16[256,4608]{1,0:T(8,128)(2,1)} %param.13) | copy-start | bytes 7077892
  6.5 127.5 %all-gather.2.cloned.1.call-start = ((), (), s32[]{:S(2)}) async-start(), calls=%async_computation.1 | async-start | bytes 20054016 | tf_op jit(solution)/shard_map/all_gather | solution.py:32
  7.3 740.2 %reduce-scatter.2.cloned.1.call-start = ((), (), s32[]{:S(2)}) async-start(), calls=%async_computation.2 | async-start | bytes 40108032 | tf_op jit(solution)/shard_map/reduce_scatter | solution.py:81
  148.9 9.4 %copy-start.11 = (bf16[1024,256]{0,1:T(8,128)(2,1)S(1)}, bf16[1024,256]{0,1:T(8,128)(2,1)}, u32[]{:S(2)}) copy-start(bf16[1024,256]{0,1:T(8,128)(2,1)} %get-tuple-element.422) | copy-start | bytes 1572868
  158.3 5.1 copy-start.9
  158.3 5.1 copy-start.10
  160.1 3.3 copy-start.8
  167.0 4.0 copy-start.12
  209.3 15.4 %collective-permute-start = (bf16[2,2,1024,1,128]{4,2,3,1,0:T(8,128)(2,1)}, bf16[2,2,1024,1,128]{4,2,3,1,0:T(8,128)(2,1)S(1)}, u32[]{:S(2)}, u32[]{:S(2)}) collective-permute-start(bf16[2,2,1024,1,128]{4,2,3,1,0:T(8,128)(2,1)} %get-tuple-element.542), channel_id=1, source_target_pairs={{0,1},{1,2},{2,3},{3,4},{4,5},{5,6},{6,7},{7,0},{8,9},{9,10},{10,1... | collective-permute-start | bytes 3145736 | tf_op jit(solution)/shard_map/while/body/eval_jaxpr/ppermute | solution.py:68
  234.6 8.6 %copy-start.1 = (f32[1,2,1024,128]{3,2,1,0:T(8,128)S(1)}, f32[1,2,1024,128]{3,2,1,0:T(8,128)}, u32[]{:S(2)}) copy-start(f32[1,2,1024,128]{3,2,1,0:T(8,128)} %get-tuple-element.328) | copy-start | bytes 3145732 | tf_op jit(solution)/shard_map/while/body/eval_jaxpr/cond
  250.6 1.0 copy-start.3
  253.2 15.4 %collective-permute-start = (bf16[2,2,1024,1,128]{4,2,3,1,0:T(8,128)(2,1)}, bf16[2,2,1024,1,128]{4,2,3,1,0:T(8,128)(2,1)S(1)}, u32[]{:S(2)}, u32[]{:S(2)}) collective-permute-start(bf16[2,2,1024,1,128]{4,2,3,1,0:T(8,128)(2,1)} %get-tuple-element.542), channel_id=1, source_target_pairs={{0,1},{1,2},{2,3},{3,4},{4,5},{5,6},{6,7},{7,0},{8,9},{9,10},{10,1... | collective-permute-start | bytes 3145736 | tf_op jit(solution)/shard_map/while/body/eval_jaxpr/ppermute | solution.py:68
  278.4 8.6 %copy-start.1 = (f32[1,2,1024,128]{3,2,1,0:T(8,128)S(1)}, f32[1,2,1024,128]{3,2,1,0:T(8,128)}, u32[]{:S(2)}) copy-start(f32[1,2,1024,128]{3,2,1,0:T(8,128)} %get-tuple-element.328) | copy-start | bytes 3145732 | tf_op jit(solution)/shard_map/while/body/eval_jaxpr/cond
  294.4 1.0 copy-start.3
  297.1 15.4 %collective-permute-start = (bf16[2,2,1024,1,128]{4,2,3,1,0:T(8,128)(2,1)}, bf16[2,2,1024,1,128]{4,2,3,1,0:T(8,128)(2,1)S(1)}, u32[]{:S(2)}, u32[]{:S(2)}) collective-permute-start(bf16[2,2,1024,1,128]{4,2,3,1,0:T(8,128)(2,1)} %get-tuple-element.542), channel_id=1, source_target_pairs={{0,1},{1,2},{2,3},{3,4},{4,5},{5,6},{6,7},{7,0},{8,9},{9,10},{10,1... | collective-permute-start | bytes 3145736 | tf_op jit(solution)/shard_map/while/body/eval_jaxpr/ppermute | solution.py:68
  322.3 8.6 %copy-start.1 = (f32[1,2,1024,128]{3,2,1,0:T(8,128)S(1)}, f32[1,2,1024,128]{3,2,1,0:T(8,128)}, u32[]{:S(2)}) copy-start(f32[1,2,1024,128]{3,2,1,0:T(8,128)} %get-tuple-element.328) | copy-start | bytes 3145732 | tf_op jit(solution)/shard_map/while/body/eval_jaxpr/cond
  341.0 15.4 %collective-permute-start = (bf16[2,2,1024,1,128]{4,2,3,1,0:T(8,128)(2,1)}, bf16[2,2,1024,1,128]{4,2,3,1,0:T(8,128)(2,1)S(1)}, u32[]{:S(2)}, u32[]{:S(2)}) collective-permute-start(bf16[2,2,1024,1,128]{4,2,3,1,0:T(8,128)(2,1)} %get-tuple-element.542), channel_id=1, source_target_pairs={{0,1},{1,2},{2,3},{3,4},{4,5},{5,6},{6,7},{7,0},{8,9},{9,10},{10,1... | collective-permute-start | bytes 3145736 | tf_op jit(solution)/shard_map/while/body/eval_jaxpr/ppermute | solution.py:68
  366.2 8.6 %copy-start.1 = (f32[1,2,1024,128]{3,2,1,0:T(8,128)S(1)}, f32[1,2,1024,128]{3,2,1,0:T(8,128)}, u32[]{:S(2)}) copy-start(f32[1,2,1024,128]{3,2,1,0:T(8,128)} %get-tuple-element.328) | copy-start | bytes 3145732 | tf_op jit(solution)/shard_map/while/body/eval_jaxpr/cond
  384.8 15.4 %collective-permute-start = (bf16[2,2,1024,1,128]{4,2,3,1,0:T(8,128)(2,1)}, bf16[2,2,1024,1,128]{4,2,3,1,0:T(8,128)(2,1)S(1)}, u32[]{:S(2)}, u32[]{:S(2)}) collective-permute-start(bf16[2,2,1024,1,128]{4,2,3,1,0:T(8,128)(2,1)} %get-tuple-element.542), channel_id=1, source_target_pairs={{0,1},{1,2},{2,3},{3,4},{4,5},{5,6},{6,7},{7,0},{8,9},{9,10},{10,1... | collective-permute-start | bytes 3145736 | tf_op jit(solution)/shard_map/while/body/eval_jaxpr/ppermute | solution.py:68
  410.1 8.6 %copy-start.1 = (f32[1,2,1024,128]{3,2,1,0:T(8,128)S(1)}, f32[1,2,1024,128]{3,2,1,0:T(8,128)}, u32[]{:S(2)}) copy-start(f32[1,2,1024,128]{3,2,1,0:T(8,128)} %get-tuple-element.328) | copy-start | bytes 3145732 | tf_op jit(solution)/shard_map/while/body/eval_jaxpr/cond
  428.7 15.4 %collective-permute-start = (bf16[2,2,1024,1,128]{4,2,3,1,0:T(8,128)(2,1)}, bf16[2,2,1024,1,128]{4,2,3,1,0:T(8,128)(2,1)S(1)}, u32[]{:S(2)}, u32[]{:S(2)}) collective-permute-start(bf16[2,2,1024,1,128]{4,2,3,1,0:T(8,128)(2,1)} %get-tuple-element.542), channel_id=1, source_target_pairs={{0,1},{1,2},{2,3},{3,4},{4,5},{5,6},{6,7},{7,0},{8,9},{9,10},{10,1... | collective-permute-start | bytes 3145736 | tf_op jit(solution)/shard_map/while/body/eval_jaxpr/ppermute | solution.py:68
  453.9 8.6 %copy-start.1 = (f32[1,2,1024,128]{3,2,1,0:T(8,128)S(1)}, f32[1,2,1024,128]{3,2,1,0:T(8,128)}, u32[]{:S(2)}) copy-start(f32[1,2,1024,128]{3,2,1,0:T(8,128)} %get-tuple-element.328) | copy-start | bytes 3145732 | tf_op jit(solution)/shard_map/while/body/eval_jaxpr/cond
  472.6 15.4 %collective-permute-start = (bf16[2,2,1024,1,128]{4,2,3,1,0:T(8,128)(2,1)}, bf16[2,2,1024,1,128]{4,2,3,1,0:T(8,128)(2,1)S(1)}, u32[]{:S(2)}, u32[]{:S(2)}) collective-permute-start(bf16[2,2,1024,1,128]{4,2,3,1,0:T(8,128)(2,1)} %get-tuple-element.542), channel_id=1, source_target_pairs={{0,1},{1,2},{2,3},{3,4},{4,5},{5,6},{6,7},{7,0},{8,9},{9,10},{10,1... | collective-permute-start | bytes 3145736 | tf_op jit(solution)/shard_map/while/body/eval_jaxpr/ppermute | solution.py:68
  497.8 8.6 %copy-start.1 = (f32[1,2,1024,128]{3,2,1,0:T(8,128)S(1)}, f32[1,2,1024,128]{3,2,1,0:T(8,128)}, u32[]{:S(2)}) copy-start(f32[1,2,1024,128]{3,2,1,0:T(8,128)} %get-tuple-element.328) | copy-start | bytes 3145732 | tf_op jit(solution)/shard_map/while/body/eval_jaxpr/cond
  (5 other events, 4.9 us)
Sparse Core Ops, SparseCore 0:
  9.5 124.5 all-gather.1
  534.2 213.2 reduce-scatter.1
where the time goes:
time: 767 us; the launch traced here: 757 us
  waiting for transfers between devices  446 us (58%)
  matrix products  191 us (25%)
  other arithmetic  85.5 us (11%)
  local copies, waits for them, and re-layouts  20.3 us (3%)
  between operations  14 us (2%)
    reduce_scatter x1, waiting for transfers between devices, local_layer(): y_loc = lax.psum_scatter(partial, 'tp', scatter_dimension=0, tiled=True)  213 us
    all_gather x1, waiting for transfers between devices, local_layer(): x_block = lax.all_gather(x_loc, 'tp', axis=0, tiled=True)  124 us
    ppermute x7, waiting for transfers between devices, kv_step(): kv_held = lax.ppermute(kv_held, 'cp', shift_pairs)  108 us
    dot_general x9, matrix products, block_scores(): jnp.einsum('qhge,khe->hgqk', q_part, k_part, preferred_element_type=jnp.f...  69 us
    reduce_sum x9, other arithmetic, merge_block(): new_sum = run_sum * rescale + p_block.sum(axis=-1)  66 us
    dot_general x9, matrix products, merge_block(): jnp.einsum('hgqk,khe->hgqe', p_block.astype(jnp.bfloat16), v_part, prefer...  64.5 us
    dot_general x1, matrix products, local_layer(): jnp.dot(x_block, w_v, preferred_element_type=jnp.float32)  24.6 us
  transfers between devices with their start and end apart: 9, of which 9 were waited for; matrix products, arithmetic and copies ran while one was open for 0% of the time, Pallas kernels for 0%

commit v1 on v0

v1 whole, which is shorter than its diff:
```python
import functools

import jax
import jax.numpy as jnp
from jax import lax
from jax.experimental import pallas as pl
from jax.experimental.pallas import tpu as pltpu
from jax.sharding import PartitionSpec as P

HEAD_DIM = 128
LOG2E = 1.4426950408889634
NT = (((1,), (1,)), ((), ()))
SUB = 512


def attention_kernel(cp_size, q_ref, kv_ref, o_ref, acc_ref, m_ref, l_ref):
    rank = lax.axis_index("cp")
    piece = q_ref.shape[0] // 2
    coef = LOG2E * HEAD_DIM ** -0.5
    group = q_ref.shape[1] // HEAD_DIM
    nsub = piece // SUB
    subs = [(g, s) for g in range(group) for s in range(nsub)]

    def lane_sum(p):
        total = p[:, 0:128]
        for c in range(1, p.shape[1] // 128):
            total = total + p[:, c * 128:(c + 1) * 128]
        return total

    def scores(half, g, s, base, width):
        qs = q_ref[pl.ds(pl.multiple_of(half * piece + s * SUB, SUB), SUB), g * HEAD_DIM:(g + 1) * HEAD_DIM]
        ks = kv_ref[pl.ds(pl.multiple_of(base, SUB), width), 0:HEAD_DIM]
        return lax.dot_general(qs, ks, NT, preferred_element_type=jnp.float32)

    def values(p, base, width):
        vs = kv_ref[pl.ds(pl.multiple_of(base, SUB), width), HEAD_DIM:2 * HEAD_DIM]
        return jnp.dot(p.astype(jnp.bfloat16), vs, preferred_element_type=jnp.float32)

    def diag(half, _):
        base = rank * 2 * piece + half * piece
        for g, s in subs:
            width = (s + 1) * SUB
            sc = scores(half, g, s, base, width)
            row = lax.broadcasted_iota(jnp.int32, (SUB, width), 0) + s * SUB
            col = lax.broadcasted_iota(jnp.int32, (SUB, width), 1)
            sc = jnp.where(row >= col, sc, -jnp.inf)
            top = jnp.max(sc, axis=1, keepdims=True) * coef
            p = jnp.exp2(sc * coef - top)
            slot = pl.ds(pl.multiple_of(half * piece + s * SUB, SUB), SUB)
            m_ref[g, slot, :] = jnp.broadcast_to(top, (SUB, 128))
            l_ref[g, slot, :] = lane_sum(p)
            acc_ref[g, slot, :] = values(p, base, width)
        return 0

    def full(job, _):
        n_high = 2 * cp_size - 1 - rank
        is_high = job < n_high
        half = jnp.where(is_high, 1, 0)
        p_idx = jnp.where(is_high, job, job - n_high)
        first = p_idx < cp_size
        base = jnp.where(first, p_idx * 2 * piece, (2 * cp_size - 1 - p_idx) * 2 * piece + piece)
        nxt = scores(half, *subs[0], base, piece)
        for i, (g, s) in enumerate(subs):
            sc = nxt
            if i + 1 < len(subs):
                nxt = scores(half, *subs[i + 1], base, piece)
            slot = pl.ds(pl.multiple_of(half * piece + s * SUB, SUB), SUB)
            m_old = m_ref[g, slot, :]
            top = jnp.max(sc, axis=1, keepdims=True) * coef
            m_new = jnp.maximum(m_old, top)
            scale = jnp.exp2(m_old - m_new)
            p = jnp.exp2(sc * coef - m_new[:, 0:1])
            m_ref[g, slot, :] = m_new
            l_ref[g, slot, :] = l_ref[g, slot, :] * scale + lane_sum(p)
            acc_ref[g, slot, :] = acc_ref[g, slot, :] * scale + values(p, base, piece)
        return 0

    lax.fori_loop(0, 2, diag, 0)
    lax.fori_loop(0, 2 * cp_size - 1, full, 0)

    def finish(i, _):
        slot = pl.ds(pl.multiple_of(i * SUB, SUB), SUB)
        for g in range(group):
            total = jnp.sum(l_ref[g, slot, :], axis=1, keepdims=True)
            o_ref[slot, g * HEAD_DIM:(g + 1) * HEAD_DIM] = (acc_ref[g, slot, :] / total).astype(jnp.bfloat16)
        return 0

    lax.fori_loop(0, 2 * nsub, finish, 0)


def attention(cp_size, q, kv):
    rows, width = q.shape
    group = width // HEAD_DIM
    flops = 4 * rows * group * HEAD_DIM * (kv.shape[0] // 2)
    vmem = pl.BlockSpec(memory_space=pltpu.VMEM)
    return pl.pallas_call(
        functools.partial(attention_kernel, cp_size),
        out_shape=jax.ShapeDtypeStruct(q.shape, jnp.bfloat16),
        in_specs=[vmem, vmem],
        out_specs=vmem,
        scratch_shapes=[pltpu.VMEM((group, rows, 128), jnp.float32) for _ in range(3)],
        compiler_params=pltpu.CompilerParams(vmem_limit_bytes=50 * 1024 * 1024),
        cost_estimate=pl.CostEstimate(flops=flops, bytes_accessed=kv.size * 2 + q.size * 4, transcendentals=flops // 512),
        name="attention",
    )(q, kv)


def solution(mesh):
    cp_size = mesh.shape["cp"]
    tp_size = mesh.shape["tp"]
    row_spec = P(("dp", "cp", "tp"), None)

    def local_layer(x_loc, w_q, w_k, w_v, w_o):
        model_width = x_loc.shape[1]
        cols = model_width // tp_size
        w_kv = jnp.concatenate([w_k, w_v], axis=1)
        w_cols = lax.all_to_all(w_o, "tp", split_axis=1, concat_axis=0, tiled=True)
        x_block = lax.all_gather(x_loc, "tp", axis=0, tiled=True)
        kv_own = jnp.dot(x_block, w_kv, preferred_element_type=jnp.float32).astype(jnp.bfloat16)
        kv_all = lax.all_gather(kv_own, "cp", axis=0, tiled=True)
        q_own = jnp.dot(x_block, w_q, preferred_element_type=jnp.float32).astype(jnp.bfloat16)
        heads = attention(cp_size, q_own, kv_all)
        heads_all = lax.all_gather(heads, "tp", axis=0, tiled=False)
        w_split = w_cols.reshape(tp_size, heads.shape[1], cols)
        y_cols = jnp.einsum("tsh,thd->sd", heads_all, w_split, preferred_element_type=jnp.float32).astype(jnp.bfloat16)
        return lax.all_to_all(y_cols, "tp", split_axis=0, concat_axis=1, tiled=True)

    return jax.shard_map(local_layer, mesh=mesh, in_specs=(row_spec, P(None, "tp"), P(None, "tp"), P(None, "tp"), P("tp", None)), out_specs=row_spec, check_vma=False)
```

time: 767 us -> 429 us (0.56); the launches traced: 757 us -> 429 us
  waiting for transfers between devices: 446 us -> 243 us
  matrix products: 191 us -> 28.9 us
  other arithmetic: 85.5 us -> 0 us
  blocking collectives: 0 us -> 78.7 us
  Pallas kernels: 0 us -> 59.2 us
  local copies, waits for them, and re-layouts: 20.3 us -> 5.89 us
    reduce_scatter x1 -> x0, waiting for transfers between devices: 213 us -> none  [local_layer(): y_loc = lax.psum_scatter(partial, 'tp', scatter_dimension=0, tiled=True)]
    dot_general x21 -> x2, matrix products: 182 us -> 19.8 us  [the longest x1 10.4 us: local_layer(): jnp.dot(x_block, w_kv, preferred_element_type=jnp.float32)]
    all_gather x0 -> x2, waiting for transfers between devices: none -> 115 us  [the longest x1 75.4 us: local_layer(): heads_all = lax.all_gather(heads, 'tp', axis=0, tiled=False)]
    ppermute x7 -> x0, waiting for transfers between devices: 108 us -> none  [kv_step(): kv_held = lax.ppermute(kv_held, 'cp', shift_pairs)]
    all_to_all x0 -> x2, blocking collectives: none -> 78.7 us  [the longest x1 55 us: local_layer(): w_cols = lax.all_to_all(w_o, 'tp', split_axis=1, concat_axis=0, tiled=True)]
    reduce_sum x9 -> x0, other arithmetic: 66 us -> none  [merge_block(): new_sum = run_sum * rescale + p_block.sum(axis=-1)]
    pallas_call x0 -> x1, Pallas kernels: none -> 59.2 us  [attention(): pl.pallas_call(functools.partial(attention_kernel, cp_size), out_shape=ja...]
    while x16 -> x0, local copies, waits for them, and re-layouts: 15.8 us -> none
  transfers between devices with their start and end apart: 9 -> 3, of which waited for: 9 -> 3; matrix products, arithmetic and copies ran while one was open for 0% -> 3% of each run, Pallas kernels for 0% -> 0%
where the time goes in v1:
time: 429 us
  waiting for transfers between devices  243 us (57%)
  blocking collectives  78.7 us (18%)
  Pallas kernels  59.2 us (14%)
  matrix products  28.9 us (7%)
  between operations  13.1 us (3%)
  local copies, waits for them, and re-layouts  5.89 us (1%)
    all_gather x1, waiting for transfers between devices, local_layer(): x_block = lax.all_gather(x_loc, 'tp', axis=0, tiled=True)  127 us
    all_gather x1, waiting for transfers between devices, local_layer(): heads_all = lax.all_gather(heads, 'tp', axis=0, tiled=False)  75.4 us
    pallas_call x1, Pallas kernels, attention(): pl.pallas_call(functools.partial(attention_kernel, cp_size), out_shape=ja...  59.2 us
    all_to_all x1, blocking collectives, local_layer(): w_cols = lax.all_to_all(w_o, 'tp', split_axis=1, concat_axis=0, tiled=True)  55 us
    all_gather x1, waiting for transfers between devices, local_layer(): kv_all = lax.all_gather(kv_own, 'cp', axis=0, tiled=True)  40 us
    all_to_all x1, blocking collectives, local_layer(): return lax.all_to_all(y_cols, 'tp', split_axis=0, concat_axis=1, tiled=True)  23.7 us
    dot_general x1, matrix products, local_layer(): jnp.dot(x_block, w_kv, preferred_element_type=jnp.float32)  10.4 us
    dot_general x1, matrix products, local_layer(): jnp.einsum('tsh,thd->sd', heads_all, w_split, preferred_element_type=jnp....  9.34 us
  transfers between devices with their start and end apart: 3, of which 3 were waited for; matrix products, arithmetic and copies ran while one was open for 3% of the time, Pallas kernels for 0%

profile of v1, /device:TPU:0, one launch (start us, length us, event | category | flops | bytes accessed | tf_op | source)
XLA Modules:
  0.0 428.7 jit_solution(5946142354279791494)
XLA Ops:
  6.5 0.0 copy-start
  6.5 0.0 all-gather.5.cloned.1.call-start
  6.5 0.7 all-gather.5.cloned.1.call-update
  7.3 0.0 all-gather.7.cloned.1.call-start
  7.3 126.7 %all-gather.5.cloned.1.call-done = bf16[2048,4608]{1,0:T(8,128)(2,1)} async-done(((bf16[128,4608]{1,0:T(8,128)(2,1)}), bf16[2048,4608]{1,0:T(8,128)(2,1)}) %all-gather.5.cloned.1.call-update) | async-done | bytes 18874384 | tf_op jit(solution)/shard_map/all_gather | solution.py:118
  134.0 10.4 %fusion.1 = bf16[2048,256]{1,0:T(8,128)(2,1)} fusion(bf16[2048,4608]{1,0:T(8,128)(2,1)} %all-gather.5.cloned.1.call-done, bf16[4608,128]{1,0:T(8,128)(2,1)} %param.8, bf16[4608,128]{1,0:T(8,128)(2,1)} %param.7), kind=kOutput, calls=%fused_computation.4 | convolution fusion | flops 4837081088 | bytes 22282240 | tf_op jit(solution)/shard_map/dot_general | solution.py:119
  144.5 0.0 all-gather.7.cloned.1.call-update
  144.5 0.0 all-gather.9.cloned.1.call-start
  144.5 0.0 copy-done
  144.5 9.1 %convolution_convert_fusion.1.q_ref = bf16[2048,256]{1,0:T(8,128)(2,1)S(1)} fusion(bf16[2048,4608]{1,0:T(8,128)(2,1)} %all-gather.5.cloned.1.call-done, bf16[4608,256]{1,0:T(8,128)(2,1)S(1)} %copy-done), kind=kOutput, calls=%fused_computation.3 | convolution fusion | flops 4832362496 | bytes 22282240 | tf_op jit(solution)/shard_map/dot_general | solution.py:121
  153.7 40.0 %all-gather.7.cloned.1.call-done.kv_ref = bf16[16384,256]{1,0:T(8,128)(2,1)} async-done(((bf16[2048,256]{1,0:T(8,128)(2,1)}), bf16[16384,256]{1,0:T(8,128)(2,1)}) %all-gather.7.cloned.1.call-update) | async-done | bytes 8388624 | tf_op jit(solution)/shard_map/all_gather | solution.py:120
  193.7 59.2 %attention.1 = bf16[2048,256]{1,0:T(8,128)(2,1)} custom-call(bf16[2048,256]{1,0:T(8,128)(2,1)S(1)} %convolution_convert_fusion.1.q_ref, bf16[16384,256]{1,0:T(8,128)(2,1)} %all-gather.7.cloned.1.call-done.kv_ref), custom_call_target="tpu_custom_call" | custom-call | flops 17179869184 | bytes 10485760 | tf_op jit(solution)/shard_map/attention/pallas_call | solution.py:96
  252.9 0.0 all-gather.9.cloned.1.call-update
  252.9 4.3 copy.10
  257.2 55.0 %all_to_all.35 = bf16[256,16,288]{0,2,1:T(8,128)(2,1)} all-to-all(bf16[256,16,288]{0,2,1:T(8,128)(2,1)} %bitcast.27), channel_id=1, replica_groups=mesh['dp'=1,'tp'=16,'cp'=8] {'tp'}, dimensions={1} | all-to-all | bytes 4718592 | tf_op jit(solution)/shard_map/all_to_all | solution.py:117
  312.2 75.4 %all-gather.9.cloned.1.call-done = bf16[32768,256]{1,0:T(8,128)(2,1)} async-done(((bf16[2048,256]{1,0:T(8,128)(2,1)}), bf16[32768,256]{1,0:T(8,128)(2,1)}) %all-gather.9.cloned.1.call-update) | async-done | bytes 16777232 | tf_op jit(solution)/shard_map/all_gather | solution.py:123
  387.6 9.3 %fusion.6 = bf16[36,16,8,128]{3,2,1,0:T(8,128)(2,1)S(1)} fusion(bf16[16,2048,256]{2,1,0:T(8,128)(2,1)} %bitcast.30, bf16[256,16,288]{0,2,1:T(8,128)(2,1)} %all_to_all.35), kind=kOutput, calls=%fused_computation.9 | convolution fusion | flops 4832428032 | bytes 20316160 | tf_op jit(solution)/shard_map/tsh,thd->sd/dot_general | solution.py:125
  396.9 0.2 copy.16
  397.1 23.7 %all_to_all.36 = bf16[16,128,288]{1,2,0:T(8,128)(2,1)S(1)} all-to-all(bf16[16,128,288]{1,2,0:T(8,128)(2,1)S(1)} %bitcast.28), channel_id=1, replica_groups=mesh['dp'=1,'tp'=16,'cp'=8] {'tp'}, dimensions={0} | all-to-all | bytes 2359296 | tf_op jit(solution)/shard_map/all_to_all | solution.py:126
  420.8 1.4 copy.12
Async XLA Ops:
  6.5 138.0 %copy-start = (bf16[4608,256]{1,0:T(8,128)(2,1)S(1)}, bf16[4608,256]{1,0:T(8,128)(2,1)}, u32[]{:S(2)}) copy-start(bf16[4608,256]{1,0:T(8,128)(2,1)} %param.6) | copy-start | bytes 7077892
  6.5 127.5 %all-gather.5.cloned.1.call-start = ((), (), s32[]{:S(2)}) async-start(), calls=%async_computation.2 | async-start | bytes 20054016 | tf_op jit(solution)/shard_map/all_gather | solution.py:118
  7.3 186.4 %all-gather.7.cloned.1.call-start = ((), (), s32[]{:S(2)}) async-start(), calls=%async_computation.3 | async-start | bytes 9437184 | tf_op jit(solution)/shard_map/all_gather | solution.py:120
  144.5 243.1 %all-gather.9.cloned.1.call-start = ((), (), s32[]{:S(2)}) async-start(), calls=%async_computation.4 | async-start | bytes 17825792 | tf_op jit(solution)/shard_map/all_gather | solution.py:123
Sparse Core Ops, SparseCore 0:
  9.5 124.5 all-gather.4
  144.6 49.0 all-gather.6
  253.0 134.5 all-gather.8

commit v2 on v1

--- a/solution.py
+++ b/solution.py
@@ -105,6 +105,172 @@
     )(q, kv)
 
 
+MESH = pl.DeviceIdType.MESH
+X_SUB = 2
+
+
+def front_kernel(tp_size, cp_size, x_hbm, wq_hbm, wk_hbm, wv_hbm, q_hbm, kv_hbm, xg, w_buf, q_buf, kv, load_sem, ring_send, ring_recv, kv_send, left_recv, right_recv, far_recv, pair_recv):
+    tp = lax.axis_index("tp")
+    cp = lax.axis_index("cp")
+    side = 4
+    zi, yi = tp // side, lax.rem(tp, side)
+    chip, core = cp // 2, lax.rem(cp, 2)
+    n_chip = cp_size // 2
+    rows = x_hbm.shape[0]
+    block = rows * tp_size
+    part = rows // 4
+    sub = part // X_SUB
+    q_width = wq_hbm.shape[1]
+    k_width = wk_hbm.shape[1]
+    pos = (zi * side + lax.rem(yi + zi, side), yi * side + lax.rem(zi + yi, side))
+
+    def member(cycle, k):
+        k = lax.rem(k + 2 * tp_size, tp_size)
+        major = k // side
+        minor = lax.rem(k - major + side, side)
+        return major * side + minor if cycle == 0 else minor * side + major
+
+    streams = [(0, 1), (0, -1), (1, 1), (1, -1)]
+    nxt = [member(c, pos[c] + d) for c, d in streams]
+    right = lax.rem(chip + 1, n_chip) * 2 + core
+    left = lax.rem(chip + n_chip - 1, n_chip) * 2 + core
+    far = lax.rem(chip + 2, n_chip) * 2 + core
+    pair = cp + 1 - 2 * core
+    ahead = jnp.where(core == 0, right, left)
+    behind = jnp.where(core == 0, left, right)
+
+    w_q = pltpu.make_async_copy(wq_hbm, w_buf.at[:, pl.ds(0, q_width)], load_sem.at[0])
+    w_k = pltpu.make_async_copy(wk_hbm, w_buf.at[:, pl.ds(q_width, k_width)], load_sem.at[1])
+    w_v = pltpu.make_async_copy(wv_hbm, w_buf.at[:, pl.ds(q_width + k_width, k_width)], load_sem.at[2])
+    own = pltpu.make_async_copy(x_hbm, xg.at[pl.ds(pl.multiple_of(tp * rows, rows), rows)], load_sem.at[3])
+    own.start()
+    w_q.start()
+    w_k.start()
+    w_v.start()
+
+    barrier = pltpu.get_barrier_semaphore()
+    for peer in nxt:
+        pl.semaphore_signal(barrier, inc=1, device_id={"tp": peer}, device_id_type=MESH)
+    for peer in (left, right, pair):
+        pl.semaphore_signal(barrier, inc=1, device_id={"cp": peer}, device_id_type=MESH)
+    pl.semaphore_wait(barrier, 7)
+    own.wait()
+
+    def source(s, t):
+        c, d = streams[s]
+        return member(c, pos[c] - d * t)
+
+    def ring(s, t, u):
+        at = xg.at[pl.ds(pl.multiple_of(source(s, t) * rows + s * part + u * sub, sub), sub)]
+        return at, dict(send_sem=ring_send.at[s], device_id={"tp": nxt[s]}, device_id_type=MESH)
+
+    def move(ref, send_sem, recv_sem, axis, peer):
+        return pltpu.make_async_remote_copy(src_ref=ref, dst_ref=ref, send_sem=send_sem, recv_sem=recv_sem, device_id={axis: peer}, device_id_type=MESH)
+
+    def kv_rows(owner, s, t):
+        return kv.at[pl.ds(pl.multiple_of(owner * block + source(s, t) * rows + s * part, part), part)]
+
+    def kv_wait(sem, count):
+        ref = kv.at[pl.ds(0, count)]
+        pltpu.make_async_remote_copy(src_ref=ref, dst_ref=ref, send_sem=kv_send.at[0], recv_sem=sem, device_id={"cp": pair}, device_id_type=MESH).wait_recv()
+
+    def step(t, _):
+        @pl.when(t < tp_size)
+        def _():
+            for u in range(X_SUB):
+                for s in range(4):
+                    at = xg.at[pl.ds(pl.multiple_of(source(s, t) * rows + s * part + u * sub, sub), sub)]
+
+                    @pl.when(t > 0)
+                    def _():
+                        move(at, ring_send.at[s], ring_recv.at[s, t - 1, u], "tp", nxt[s]).wait_recv()
+
+                    @pl.when(t < tp_size - 1)
+                    def _():
+                        move(at, ring_send.at[s], ring_recv.at[s, t, u], "tp", nxt[s]).start()
+
+        @pl.when(jnp.logical_and(t >= 1, t <= tp_size))
+        def _():
+            for s in range(4):
+                at = kv_rows(cp, s, t - 1)
+                move(at, kv_send.at[0], left_recv.at[t - 1], "cp", right).start()
+                move(at, kv_send.at[1], right_recv.at[t - 1], "cp", left).start()
+                move(at, kv_send.at[2], pair_recv.at[0], "cp", pair).start()
+
+        @pl.when(jnp.logical_and(t >= 3, t <= tp_size + 2))
+        def _():
+            kv_wait(left_recv.at[t - 3], rows)
+            kv_wait(right_recv.at[t - 3], rows)
+            for s in range(4):
+                move(kv_rows(behind, s, t - 3), kv_send.at[3], far_recv.at[t - 3], "cp", ahead).start()
+                move(kv_rows(left, s, t - 3), kv_send.at[4], pair_recv.at[1], "cp", pair).start()
+                move(kv_rows(right, s, t - 3), kv_send.at[5], pair_recv.at[2], "cp", pair).start()
+
+        @pl.when(t >= 5)
+        def _():
+            kv_wait(far_recv.at[t - 5], rows)
+            for s in range(4):
+                move(kv_rows(far, s, t - 5), kv_send.at[6], pair_recv.at[3], "cp", pair).start()
+
+        @pl.when(t == 0)
+        def _():
+            w_q.wait()
+            w_k.wait()
+            w_v.wait()
+
+        @pl.when(t < tp_size)
+        def _():
+            offs = [pl.multiple_of(source(s, t) * rows + s * part, part) for s in range(4)]
+            lhs = jnp.concatenate([xg[pl.ds(o, part), :] for o in offs], axis=0)
+            res = jnp.dot(lhs, w_buf[...], preferred_element_type=jnp.float32).astype(jnp.bfloat16)
+            for s in range(4):
+                q_buf[pl.ds(offs[s], part), :] = res[s * part:(s + 1) * part, 0:q_width]
+                kv[pl.ds(pl.multiple_of(cp * block + offs[s], part), part), :] = res[s * part:(s + 1) * part, q_width:]
+        return 0
+
+    lax.fori_loop(0, tp_size + 5, step, 0)
+
+    for k in range(4):
+        kv_wait(pair_recv.at[k], block)
+    out_q = pltpu.make_async_copy(q_buf, q_hbm, load_sem.at[0])
+    out_kv = pltpu.make_async_copy(kv, kv_hbm, load_sem.at[1])
+    out_q.start()
+    out_kv.start()
+    for s in range(4):
+        ref = xg.at[pl.ds(0, (tp_size - 1) * part)]
+        pltpu.make_async_remote_copy(src_ref=ref, dst_ref=ref, send_sem=ring_send.at[s], recv_sem=ring_recv.at[s, 0, 0], device_id={"tp": nxt[s]}, device_id_type=MESH).wait_send()
+    for k in range(7):
+        ref = kv.at[pl.ds(0, block)]
+        pltpu.make_async_remote_copy(src_ref=ref, dst_ref=ref, send_sem=kv_send.at[k], recv_sem=pair_recv.at[0], device_id={"cp": pair}, device_id_type=MESH).wait_send()
+    out_q.wait()
+    out_kv.wait()
+
+
+def front(tp_size, cp_size, x_loc, w_q, w_k, w_v):
+    rows, depth = x_loc.shape
+    block = rows * tp_size
+    q_width = w_q.shape[1]
+    kv_width = w_k.shape[1] + w_v.shape[1]
+    any_space = pl.BlockSpec(memory_space=pl.ANY)
+    dma = pltpu.SemaphoreType.DMA
+    return pl.pallas_call(
+        functools.partial(front_kernel, tp_size, cp_size),
+        out_shape=(jax.ShapeDtypeStruct((block, q_width), jnp.bfloat16), jax.ShapeDtypeStruct((block * cp_size, kv_width), jnp.bfloat16)),
+        in_specs=[any_space] * 4,
+        out_specs=(any_space, any_space),
+        scratch_shapes=[
+            pltpu.VMEM((block, depth), jnp.bfloat16),
+            pltpu.VMEM((depth, q_width + kv_width), jnp.bfloat16),
+            pltpu.VMEM((block, q_width), jnp.bfloat16),
+            pltpu.VMEM((block * cp_size, kv_width), jnp.bfloat16),
+            dma((4,)), dma((4,)), dma((4, tp_size - 1, X_SUB)), dma((7,)), dma((tp_size,)), dma((tp_size,)), dma((tp_size,)), dma((4,)),
+        ],
+        compiler_params=pltpu.CompilerParams(collective_id=0, has_side_effects=True, vmem_limit_bytes=56 * 1024 * 1024),
+        cost_estimate=pl.CostEstimate(flops=2 * block * depth * (q_width + kv_width), bytes_accessed=block * depth * 2, transcendentals=0),
+        name="front",
+    )(x_loc, w_q, w_k, w_v)
+
+
 def solution(mesh):
     cp_size = mesh.shape["cp"]
     tp_size = mesh.shape["tp"]
@@ -113,12 +279,8 @@
     def local_layer(x_loc, w_q, w_k, w_v, w_o):
         model_width = x_loc.shape[1]
         cols = model_width // tp_size
-        w_kv = jnp.concatenate([w_k, w_v], axis=1)
         w_cols = lax.all_to_all(w_o, "tp", split_axis=1, concat_axis=0, tiled=True)
-        x_block = lax.all_gather(x_loc, "tp", axis=0, tiled=True)
-        kv_own = jnp.dot(x_block, w_kv, preferred_element_type=jnp.float32).astype(jnp.bfloat16)
-        kv_all = lax.all_gather(kv_own, "cp", axis=0, tiled=True)
-        q_own = jnp.dot(x_block, w_q, preferred_element_type=jnp.float32).astype(jnp.bfloat16)
+        q_own, kv_all = front(tp_size, cp_size, x_loc, w_q, w_k, w_v)
         heads = attention(cp_size, q_own, kv_all)
         heads_all = lax.all_gather(heads, "tp", axis=0, tiled=False)
         w_split = w_cols.reshape(tp_size, heads.shape[1], cols)

time: 429 us -> 358 us (0.83)
  waiting for transfers between devices: 243 us -> 74.2 us
  Pallas kernels: 59.2 us -> 177 us
  matrix products: 28.9 us -> 9.34 us
    all_gather x2 -> x0, waiting for transfers between devices: 167 us -> none  [the longest x1 127 us: local_layer(): x_block = lax.all_gather(x_loc, 'tp', axis=0, tiled=True)]
    pallas_call x0 -> x1, Pallas kernels: none -> 118 us  [front(): pl.pallas_call(functools.partial(front_kernel, tp_size, cp_size), out_sha...]
    dot_general x2 -> x0, matrix products: 19.5 us -> none  [the longest x1 10.4 us: local_layer(): jnp.dot(x_block, w_kv, preferred_element_type=jnp.float32)]
  transfers between devices with their start and end apart: 3 -> 1, of which waited for: 3 -> 1; matrix products, arithmetic and copies ran while one was open for 3% -> 1% of each run, Pallas kernels for 0% -> 0%
where the time goes in v2:
time: 358 us; the launch traced here: 357 us
  Pallas kernels  177 us (49%)
  blocking collectives  77.8 us (22%)
  waiting for transfers between devices  74.2 us (21%)
  between operations  13.4 us (4%)
  matrix products  9.34 us (3%)
  local copies, waits for them, and re-layouts  5.65 us (2%)
    pallas_call x1, Pallas kernels, front(): pl.pallas_call(functools.partial(front_kernel, tp_size, cp_size), out_sha...  118 us
    all_gather x1, waiting for transfers between devices, local_layer(): heads_all = lax.all_gather(heads, 'tp', axis=0, tiled=False)  74.2 us
    pallas_call x1, Pallas kernels, attention(): pl.pallas_call(functools.partial(attention_kernel, cp_size), out_shape=ja...  59.2 us
    all_to_all x1, blocking collectives, local_layer(): w_cols = lax.all_to_all(w_o, 'tp', split_axis=1, concat_axis=0, tiled=True)  54.1 us
    all_to_all x1, blocking collectives, local_layer(): return lax.all_to_all(y_cols, 'tp', split_axis=0, concat_axis=1, tiled=True)  23.7 us
    dot_general x1, matrix products, local_layer(): jnp.einsum('tsh,thd->sd', heads_all, w_split, preferred_element_type=jnp....  9.34 us
  transfers between devices with their start and end apart: 1, of which 1 were waited for; matrix products, arithmetic and copies ran while one was open for 1% of the time, Pallas kernels for 0%

profile of v2, /device:TPU:0, one launch (start us, length us, event | category | flops | bytes accessed | tf_op | source)
XLA Modules:
  0.0 357.4 jit_solution(15600940496068707475)
XLA Ops:
  6.5 0.0 all-gather.3.cloned.1.call-start
  6.5 117.7 %front.1 = (bf16[2048,256]{1,0:T(8,128)(2,1)}, bf16[16384,256]{1,0:T(8,128)(2,1)}) custom-call(bf16[128,4608]{1,0:T(8,128)(2,1)} %x_hbm.1, bf16[4608,256]{1,0:T(8,128)(2,1)} %wq_hbm.1, bf16[4608,128]{1,0:T(8,128)(2,1)} %wk_hbm.1, bf16[4608,128]{1,0:T(8,128)(2,1)} %wv_hbm.1), custom_call_target="tpu_custom_call" | custom-call | flops 9663676416 | bytes 18874368 | tf_op jit(solution)/shard_map/front/pallas_call | solution.py:256
  124.3 0.0 copy-start
  124.3 1.2 copy-done
  125.5 59.2 %attention.1 = bf16[2048,256]{1,0:T(8,128)(2,1)} custom-call(bf16[2048,256]{1,0:T(8,128)(2,1)S(1)} %copy-done, bf16[16384,256]{1,0:T(8,128)(2,1)} %get-tuple-element.8.kv_ref), custom_call_target="tpu_custom_call" | custom-call | flops 17179869184 | bytes 10485760 | tf_op jit(solution)/shard_map/attention/pallas_call | solution.py:96
  184.7 0.0 all-gather.3.cloned.1.call-update
  184.7 2.8 copy.8
  187.6 54.1 %all_to_all.35 = bf16[256,16,288]{0,2,1:T(8,128)(2,1)} all-to-all(bf16[256,16,288]{0,2,1:T(8,128)(2,1)S(1)} %bitcast.22), channel_id=1, replica_groups=mesh['dp'=1,'tp'=16,'cp'=8] {'tp'}, dimensions={1} | all-to-all | bytes 4718592 | tf_op jit(solution)/shard_map/all_to_all | solution.py:282
  241.7 74.2 %all-gather.3.cloned.1.call-done = bf16[32768,256]{1,0:T(8,128)(2,1)} async-done(((bf16[2048,256]{1,0:T(8,128)(2,1)}), bf16[32768,256]{1,0:T(8,128)(2,1)}) %all-gather.3.cloned.1.call-update) | async-done | bytes 16777232 | tf_op jit(solution)/shard_map/all_gather | solution.py:285
  315.8 9.3 %fusion.2 = bf16[36,16,8,128]{3,2,1,0:T(8,128)(2,1)S(1)} fusion(bf16[16,2048,256]{2,1,0:T(8,128)(2,1)} %bitcast.25, bf16[256,16,288]{0,2,1:T(8,128)(2,1)} %all_to_all.35), kind=kOutput, calls=%fused_computation.3 | convolution fusion | flops 4832428032 | bytes 20316160 | tf_op jit(solution)/shard_map/tsh,thd->sd/dot_general | solution.py:287
  325.2 0.2 copy.13
  325.4 23.7 %all_to_all.36 = bf16[16,128,288]{1,2,0:T(8,128)(2,1)S(1)} all-to-all(bf16[16,128,288]{1,2,0:T(8,128)(2,1)S(1)} %bitcast.23), channel_id=1, replica_groups=mesh['dp'=1,'tp'=16,'cp'=8] {'tp'}, dimensions={0} | all-to-all | bytes 2359296 | tf_op jit(solution)/shard_map/all_to_all | solution.py:288
  349.1 1.4 copy.10
Async XLA Ops:
  6.5 309.3 %all-gather.3.cloned.1.call-start = ((), (), s32[]{:S(2)}) async-start(), calls=%async_computation.2 | async-start | bytes 17825792 | tf_op jit(solution)/shard_map/all_gather | solution.py:285
  124.3 1.2 copy-start
Sparse Core Ops, SparseCore 0:
  184.8 130.9 all-gather.2

commit v3 on v2

--- a/solution.py
+++ b/solution.py
@@ -11,98 +11,6 @@
 LOG2E = 1.4426950408889634
 NT = (((1,), (1,)), ((), ()))
 SUB = 512
-
-
-def attention_kernel(cp_size, q_ref, kv_ref, o_ref, acc_ref, m_ref, l_ref):
-    rank = lax.axis_index("cp")
-    piece = q_ref.shape[0] // 2
-    coef = LOG2E * HEAD_DIM ** -0.5
-    group = q_ref.shape[1] // HEAD_DIM
-    nsub = piece // SUB
-    subs = [(g, s) for g in range(group) for s in range(nsub)]
-
-    def lane_sum(p):
-        total = p[:, 0:128]
-        for c in range(1, p.shape[1] // 128):
-            total = total + p[:, c * 128:(c + 1) * 128]
-        return total
-
-    def scores(half, g, s, base, width):
-        qs = q_ref[pl.ds(pl.multiple_of(half * piece + s * SUB, SUB), SUB), g * HEAD_DIM:(g + 1) * HEAD_DIM]
-        ks = kv_ref[pl.ds(pl.multiple_of(base, SUB), width), 0:HEAD_DIM]
-        return lax.dot_general(qs, ks, NT, preferred_element_type=jnp.float32)
-
-    def values(p, base, width):
-        vs = kv_ref[pl.ds(pl.multiple_of(base, SUB), width), HEAD_DIM:2 * HEAD_DIM]
-        return jnp.dot(p.astype(jnp.bfloat16), vs, preferred_element_type=jnp.float32)
-
-    def diag(half, _):
-        base = rank * 2 * piece + half * piece
-        for g, s in subs:
-            width = (s + 1) * SUB
-            sc = scores(half, g, s, base, width)
-            row = lax.broadcasted_iota(jnp.int32, (SUB, width), 0) + s * SUB
-            col = lax.broadcasted_iota(jnp.int32, (SUB, width), 1)
-            sc = jnp.where(row >= col, sc, -jnp.inf)
-            top = jnp.max(sc, axis=1, keepdims=True) * coef
-            p = jnp.exp2(sc * coef - top)
-            slot = pl.ds(pl.multiple_of(half * piece + s * SUB, SUB), SUB)
-            m_ref[g, slot, :] = jnp.broadcast_to(top, (SUB, 128))
-            l_ref[g, slot, :] = lane_sum(p)
-            acc_ref[g, slot, :] = values(p, base, width)
-        return 0
-
-    def full(job, _):
-        n_high = 2 * cp_size - 1 - rank
-        is_high = job < n_high
-        half = jnp.where(is_high, 1, 0)
-        p_idx = jnp.where(is_high, job, job - n_high)
-        first = p_idx < cp_size
-        base = jnp.where(first, p_idx * 2 * piece, (2 * cp_size - 1 - p_idx) * 2 * piece + piece)
-        nxt = scores(half, *subs[0], base, piece)
-        for i, (g, s) in enumerate(subs):
-            sc = nxt
-            if i + 1 < len(subs):
-                nxt = scores(half, *subs[i + 1], base, piece)
-            slot = pl.ds(pl.multiple_of(half * piece + s * SUB, SUB), SUB)
-            m_old = m_ref[g, slot, :]
-            top = jnp.max(sc, axis=1, keepdims=True) * coef
-            m_new = jnp.maximum(m_old, top)
-            scale = jnp.exp2(m_old - m_new)
-            p = jnp.exp2(sc * coef - m_new[:, 0:1])
-            m_ref[g, slot, :] = m_new
-            l_ref[g, slot, :] = l_ref[g, slot, :] * scale + lane_sum(p)
-            acc_ref[g, slot, :] = acc_ref[g, slot, :] * scale + values(p, base, piece)
-        return 0
-
-    lax.fori_loop(0, 2, diag, 0)
-    lax.fori_loop(0, 2 * cp_size - 1, full, 0)
-
-    def finish(i, _):
-        slot = pl.ds(pl.multiple_of(i * SUB, SUB), SUB)
-        for g in range(group):
-            total = jnp.sum(l_ref[g, slot, :], axis=1, keepdims=True)
-            o_ref[slot, g * HEAD_DIM:(g + 1) * HEAD_DIM] = (acc_ref[g, slot, :] / total).astype(jnp.bfloat16)
-        return 0
-
-    lax.fori_loop(0, 2 * nsub, finish, 0)
-
-
-def attention(cp_size, q, kv):
-    rows, width = q.shape
-    group = width // HEAD_DIM
-    flops = 4 * rows * group * HEAD_DIM * (kv.shape[0] // 2)
-    vmem = pl.BlockSpec(memory_space=pltpu.VMEM)
-    return pl.pallas_call(
-        functools.partial(attention_kernel, cp_size),
-        out_shape=jax.ShapeDtypeStruct(q.shape, jnp.bfloat16),
-        in_specs=[vmem, vmem],
-        out_specs=vmem,
-        scratch_shapes=[pltpu.VMEM((group, rows, 128), jnp.float32) for _ in range(3)],
-        compiler_params=pltpu.CompilerParams(vmem_limit_bytes=50 * 1024 * 1024),
-        cost_estimate=pl.CostEstimate(flops=flops, bytes_accessed=kv.size * 2 + q.size * 4, transcendentals=flops // 512),
-        name="attention",
-    )(q, kv)
 
 
 MESH = pl.DeviceIdType.MESH
@@ -271,20 +179,323 @@
     )(x_loc, w_q, w_k, w_v)
 
 
+def back_kernel(tp_size, cp_size, q_hbm, kv_hbm, wo_hbm, y_hbm, q_ref, kv_ref, w_buf, wo_buf, og, o_buf, y_send, y_all, acc_ref, m_ref, l_ref, load_sem, w_send, w_recv, d1_send, d1_recv, d2_send, d2_recv, d3_send, d3_recv):
+    side = 4
+    tp = lax.axis_index("tp")
+    rank = lax.axis_index("cp")
+    zi, yi = tp // side, lax.rem(tp, side)
+    chip, core = rank // 2, lax.rem(rank, 2)
+    n_chip = cp_size // 2
+    piece = q_ref.shape[0] // 2
+    group = q_ref.shape[1] // HEAD_DIM
+    chunk = SUB // side
+    slab = wo_buf.shape[0]
+    head_rows = slab * cp_size
+    cols = w_buf.shape[1]
+    coef = LOG2E * HEAD_DIM ** -0.5
+    right = lax.rem(chip + 1, n_chip) * 2 + core
+    left = lax.rem(chip + n_chip - 1, n_chip) * 2 + core
+    far = lax.rem(chip + 2, n_chip) * 2 + core
+    pair = rank + 1 - 2 * core
+    ahead = jnp.where(core == 0, right, left)
+    behind = jnp.where(core == 0, left, right)
+    up = lax.rem(zi + 1, side)
+    down = lax.rem(zi + side - 1, side)
+    z_far = lax.rem(zi + 2, side)
+
+    load_q = pltpu.make_async_copy(q_hbm, q_ref, load_sem.at[0])
+    load_kv = pltpu.make_async_copy(kv_hbm, kv_ref, load_sem.at[1])
+    load_w = pltpu.make_async_copy(wo_hbm.at[pl.ds(pl.multiple_of(rank * slab, slab), slab)], wo_buf, load_sem.at[2])
+    load_w.start()
+    load_q.start()
+    load_kv.start()
+    barrier = pltpu.get_barrier_semaphore()
+    for k in range(1, tp_size):
+        pl.semaphore_signal(barrier, inc=1, device_id={"tp": lax.rem(tp + k, tp_size)}, device_id_type=MESH)
+    for peer in (left, right, pair):
+        pl.semaphore_signal(barrier, inc=1, device_id={"cp": peer}, device_id_type=MESH)
+    pl.semaphore_wait(barrier, tp_size + 2)
+
+    def move(src, dst, send_sem, recv_sem, axis, peer):
+        return pltpu.make_async_remote_copy(src_ref=src, dst_ref=dst, send_sem=send_sem, recv_sem=recv_sem, device_id={axis: peer}, device_id_type=MESH)
+
+    def got(ref, recv_sem):
+        move(ref, ref, w_send.at[0], recv_sem, "cp", pair).wait_recv()
+
+    def sent(ref, send_sem):
+        move(ref, ref, send_sem, w_recv.at[0], "cp", pair).wait_send()
+
+    def w_rows(owner, member):
+        return w_buf.at[pl.ds(pl.multiple_of(owner * head_rows + member * slab, slab), slab)]
+
+    def w_cols(quarter):
+        return wo_buf.at[:, pl.ds(pl.multiple_of(quarter * cols, 128), cols)]
+
+    load_w.wait()
+    own_w = pltpu.make_async_copy(w_cols(zi), w_rows(tp, rank), load_sem.at[2])
+    own_w.start()
+
+    def spread(k, _):
+        peer = lax.rem(tp + k, tp_size)
+        move(w_cols(peer // side), w_rows(tp, rank), w_send.at[0], w_recv.at[0], "tp", peer).start()
+        return 0
+
+    lax.fori_loop(1, tp_size, spread, 0)
+
+    def w_share():
+        own_w.wait()
+        got(w_buf.at[pl.ds(0, (tp_size - 1) * slab)], w_recv.at[0])
+
+        def one(s, _):
+            ref = w_rows(s, rank)
+            move(ref, ref, w_send.at[1], w_recv.at[1], "cp", right).start()
+            move(ref, ref, w_send.at[2], w_recv.at[2], "cp", left).start()
+            move(ref, ref, w_send.at[3], w_recv.at[4], "cp", pair).start()
+            return 0
+
+        lax.fori_loop(0, tp_size, one, 0)
+
+    w_part = w_buf.at[pl.ds(0, tp_size * slab)]
+
+    def w_pass():
+        got(w_part, w_recv.at[1])
+        got(w_part, w_recv.at[2])
+
+        def one(s, _):
+            ref = w_rows(s, behind)
+            move(ref, ref, w_send.at[4], w_recv.at[3], "cp", ahead).start()
+            ref = w_rows(s, left)
+            move(ref, ref, w_send.at[5], w_recv.at[5], "cp", pair).start()
+            ref = w_rows(s, right)
+            move(ref, ref, w_send.at[6], w_recv.at[6], "cp", pair).start()
+            return 0
+
+        lax.fori_loop(0, tp_size, one, 0)
+
+    def w_last():
+        got(w_part, w_recv.at[3])
+
+        def one(s, _):
+            ref = w_rows(s, far)
+            move(ref, ref, w_send.at[7], w_recv.at[7], "cp", pair).start()
+            return 0
+
+        lax.fori_loop(0, tp_size, one, 0)
+
+    def lane_sum(p):
+        total = p[:, 0:128]
+        for c in range(1, p.shape[1] // 128):
+            total = total + p[:, c * 128:(c + 1) * 128]
+        return total
+
+    def scores(i, g, base, width):
+        qs = q_ref[pl.ds(pl.multiple_of(i * SUB, SUB), SUB), g * HEAD_DIM:(g + 1) * HEAD_DIM]
+        ks = kv_ref[pl.ds(pl.multiple_of(base, SUB), width), 0:HEAD_DIM]
+        return lax.dot_general(qs, ks, NT, preferred_element_type=jnp.float32)
+
+    def values(p, base, width):
+        vs = kv_ref[pl.ds(pl.multiple_of(base, SUB), width), HEAD_DIM:2 * HEAD_DIM]
+        return jnp.dot(p.astype(jnp.bfloat16), vs, preferred_element_type=jnp.float32)
+
+    def diag(i, s):
+        width = (s + 1) * SUB
+        base = rank * 2 * piece + (i // 2) * piece
+        for g in range(group):
+            sc = scores(i, g, base, width)
+            row = lax.broadcasted_iota(jnp.int32, (SUB, width), 0) + s * SUB
+            col = lax.broadcasted_iota(jnp.int32, (SUB, width), 1)
+            sc = jnp.where(row >= col, sc, -jnp.inf)
+            top = jnp.max(sc, axis=1, keepdims=True) * coef
+            p = jnp.exp2(sc * coef - top)
+            m_ref[g] = jnp.broadcast_to(top, (SUB, 128))
+            l_ref[g] = lane_sum(p)
+            acc_ref[g] = values(p, base, width)
+
+    def d1(i, k):
+        peer = lax.rem(yi + k, side)
+        return move(o_buf.at[i, peer], og.at[i, tp], d1_send.at[0], d1_recv.at[i], "tp", zi * side + peer)
+
+    def tile_part(i, z, half):
+        return og.at[i, pl.ds(z * side, side), pl.ds(half * (chunk // 2), chunk // 2)]
+
+    def d2(i, z, half, send, recv, peer):
+        ref = tile_part(i, z, half)
+        return move(ref, ref, d2_send.at[send], d2_recv.at[i, recv], "tp", peer * side + yi)
+
+    def gather_start(i):
+        got(og.at[i, pl.ds(0, side - 1)], d1_recv.at[i])
+        d2(i, zi, 0, 0, 0, up).start()
+        d2(i, zi, 1, 1, 2, down).start()
+        d2(i, zi, 1, 0, 1, up).start()
+        d2(i, zi, 0, 1, 3, down).start()
+
+    def gather_pass(i):
+        got(tile_part(i, down, 0), d2_recv.at[i, 0])
+        d2(i, down, 0, 2, 4, up).start()
+        got(tile_part(i, up, 1), d2_recv.at[i, 2])
+        d2(i, up, 1, 3, 5, down).start()
+
+    def gather_end(i):
+        got(tile_part(i, down, 1), d2_recv.at[i, 1])
+        got(tile_part(i, up, 0), d2_recv.at[i, 3])
+        got(tile_part(i, z_far, 0), d2_recv.at[i, 4])
+        got(tile_part(i, z_far, 1), d2_recv.at[i, 5])
+
+    y_mine = y_all.at[:, pl.ds(pl.multiple_of(zi * cols, 128), cols)]
+
+    def project(i):
+        lhs = jnp.concatenate([og[i, s] for s in range(tp_size)], axis=1)
+        y_send[i] = jnp.dot(lhs, w_buf[...], preferred_element_type=jnp.float32).astype(jnp.bfloat16)
+
+    def deliver(i):
+        @pl.when(zi != i)
+        def _():
+            move(y_send.at[i], y_mine, d3_send.at[0], d3_recv.at[0], "tp", i * side + yi).start()
+
+        @pl.when(zi == i)
+        def _():
+            y_all[:, pl.ds(pl.multiple_of(zi * cols, 128), cols)] = y_send[i]
+
+    load_q.wait()
+    load_kv.wait()
+
+    def tile(i, _):
+        is_low = i < 2
+        count = jnp.where(is_low, rank, 2 * cp_size - 1 - rank)
+        before = jnp.where(is_low, i * rank, 2 * rank + (i - 2) * (2 * cp_size - 1 - rank))
+
+        @pl.when(lax.rem(i, 2) == 0)
+        def _():
+            diag(i, 0)
+
+        @pl.when(lax.rem(i, 2) == 1)
+        def _():
+            diag(i, 1)
+
+        @pl.when(i == 2)
+        def _():
+            gather_start(0)
+            gather_start(1)
+
+        @pl.when(i == 3)
+        def _():
+            gather_start(2)
+
+        def full(j, _):
+            first = j < cp_size
+            base = jnp.where(first, j * 2 * piece, (2 * cp_size - 1 - j) * 2 * piece + piece)
+            turn = before + j
+            pl.when(turn == 10)(w_share)
+            pl.when(turn == 22)(w_pass)
+            pl.when(turn == 28)(w_last)
+            nxt = scores(i, 0, base, piece)
+            for g in range(group):
+                sc = nxt
+                if g + 1 < group:
+                    nxt = scores(i, g + 1, base, piece)
+                m_old = m_ref[g]
+                top = jnp.max(sc, axis=1, keepdims=True) * coef
+                m_new = jnp.maximum(m_old, top)
+                scale = jnp.exp2(m_old - m_new)
+                p = jnp.exp2(sc * coef - m_new[:, 0:1])
+                m_ref[g] = m_new
+                l_ref[g] = l_ref[g] * scale + lane_sum(p)
+                acc_ref[g] = acc_ref[g] * scale + values(p, base, piece)
+            return 0
+
+        early = jnp.minimum(count, 6)
+        lax.fori_loop(0, early, full, 0)
+
+        @pl.when(i == 2)
+        def _():
+            gather_pass(0)
+            gather_pass(1)
+
+        @pl.when(i == 3)
+        def _():
+            gather_pass(2)
+
+        lax.fori_loop(early, count, full, 0)
+        for g in range(group):
+            total = jnp.sum(l_ref[g], axis=1, keepdims=True)
+            out = (acc_ref[g] / total).astype(jnp.bfloat16)
+            for k in range(side):
+                o_buf[i, k, :, g * HEAD_DIM:(g + 1) * HEAD_DIM] = out[k * chunk:(k + 1) * chunk]
+        og[i, tp] = o_buf[i, yi]
+        for k in range(1, side):
+            d1(i, k).start()
+        return 0
+
+    lax.fori_loop(0, side, tile, 0)
+
+    gather_start(3)
+    for k in range(4, 8):
+        got(w_part, w_recv.at[k])
+    for i in range(3):
+        gather_end(i)
+    lax.fori_loop(0, 3, lambda i, c: (project(i), c)[1], 0)
+    gather_pass(3)
+    for i in range(3):
+        deliver(i)
+    gather_end(3)
+    project(3)
+    deliver(3)
+    got(y_all.at[:, pl.ds(0, 3 * cols)], d3_recv.at[0])
+    out = pltpu.make_async_copy(y_all, y_hbm, load_sem.at[0])
+    out.start()
+    sent(w_buf.at[pl.ds(0, (tp_size - 1) * slab)], w_send.at[0])
+    for k in range(1, 8):
+        sent(w_part, w_send.at[k])
+    sent(o_buf.at[:, pl.ds(0, side - 1)], d1_send.at[0])
+    sent(og.at[:, pl.ds(0, side)], d2_send.at[0])
+    sent(og.at[:, pl.ds(0, side)], d2_send.at[1])
+    sent(og.at[:, pl.ds(0, side), pl.ds(0, chunk // 2)], d2_send.at[2])
+    sent(og.at[:, pl.ds(0, side), pl.ds(0, chunk // 2)], d2_send.at[3])
+    sent(y_send.at[pl.ds(0, 3)], d3_send.at[0])
+    out.wait()
+
+
+def back(tp_size, cp_size, q, kv, w_o):
+    rows, width = q.shape
+    group = width // HEAD_DIM
+    model_width = w_o.shape[1]
+    side = 4
+    cols = model_width // side
+    chunk = rows // tp_size
+    any_space = pl.BlockSpec(memory_space=pl.ANY)
+    dma = pltpu.SemaphoreType.DMA
+    bf16 = jnp.bfloat16
+    flops = 4 * rows * width * (kv.shape[0] // 2) + 2 * rows * width * model_width
+    return pl.pallas_call(
+        functools.partial(back_kernel, tp_size, cp_size),
+        out_shape=jax.ShapeDtypeStruct((chunk, model_width), bf16),
+        in_specs=[any_space] * 3,
+        out_specs=any_space,
+        scratch_shapes=[
+            pltpu.VMEM((rows, width), bf16),
+            pltpu.VMEM(kv.shape, bf16),
+            pltpu.VMEM((w_o.shape[0] * tp_size, cols), bf16),
+            pltpu.VMEM((w_o.shape[0] // cp_size, model_width), bf16),
+            pltpu.VMEM((side, tp_size, chunk, width), bf16),
+            pltpu.VMEM((side, side, chunk, width), bf16),
+            pltpu.VMEM((side, chunk, cols), bf16),
+            pltpu.VMEM((chunk, model_width), bf16),
+        ] + [pltpu.VMEM((group, SUB, 128), jnp.float32) for _ in range(3)] + [
+            dma((3,)), dma((8,)), dma((8,)), dma((1,)), dma((side,)), dma((4,)), dma((side, 6)), dma((1,)), dma((1,)),
+        ],
+        compiler_params=pltpu.CompilerParams(collective_id=1, has_side_effects=True, vmem_limit_bytes=56 * 1024 * 1024),
+        cost_estimate=pl.CostEstimate(flops=flops, bytes_accessed=kv.size * 2, transcendentals=flops // 512),
+        name="back",
+    )(q, kv, w_o)
+
+
 def solution(mesh):
     cp_size = mesh.shape["cp"]
     tp_size = mesh.shape["tp"]
     row_spec = P(("dp", "cp", "tp"), None)
 
     def local_layer(x_loc, w_q, w_k, w_v, w_o):
-        model_width = x_loc.shape[1]
-        cols = model_width // tp_size
-        w_cols = lax.all_to_all(w_o, "tp", split_axis=1, concat_axis=0, tiled=True)
         q_own, kv_all = front(tp_size, cp_size, x_loc, w_q, w_k, w_v)
-        heads = attention(cp_size, q_own, kv_all)
-        heads_all = lax.all_gather(heads, "tp", axis=0, tiled=False)
-        w_split = w_cols.reshape(tp_size, heads.shape[1], cols)
-        y_cols = jnp.einsum("tsh,thd->sd", heads_all, w_split, preferred_element_type=jnp.float32).astype(jnp.bfloat16)
-        return lax.all_to_all(y_cols, "tp", split_axis=0, concat_axis=1, tiled=True)
+        return back(tp_size, cp_size, q_own, kv_all, w_o)
 
     return jax.shard_map(local_layer, mesh=mesh, in_specs=(row_spec, P(None, "tp"), P(None, "tp"), P(None, "tp"), P("tp", None)), out_specs=row_spec, check_vma=False)

time: 358 us -> 239 us (0.67)
  blocking collectives: 77.8 us -> 0 us
  waiting for transfers between devices: 74.2 us -> 0 us
  Pallas kernels: 177 us -> 235 us
  between operations: 13.4 us -> 0.02 us
  matrix products: 9.34 us -> 0 us
    all_to_all x2 -> x0, blocking collectives: 77.8 us -> none  [the longest x1 54.1 us: local_layer(): w_cols = lax.all_to_all(w_o, 'tp', split_axis=1, concat_axis=0, tiled=True)]
    all_gather x1 -> x0, waiting for transfers between devices: 74.2 us -> none  [local_layer(): heads_all = lax.all_gather(heads, 'tp', axis=0, tiled=False)]
    pallas_call x1, Pallas kernels: 59.2 us -> 117 us  [back(): pl.pallas_call(functools.partial(back_kernel, tp_size, cp_size), out_shap...]
    dot_general x1 -> x0, matrix products: 9.34 us -> none  [local_layer(): jnp.einsum('tsh,thd->sd', heads_all, w_split, preferred_element_type=jnp....]
  transfers between devices with their start and end apart: 1 -> 0, of which waited for: 1 -> 0; matrix products, arithmetic and copies ran while one was open for 1% -> 0% of each run, Pallas kernels for 0% -> 0%
where the time goes in v3:
time: 239 us; the launch traced here: 238 us
  Pallas kernels  235 us (98%)
    pallas_call x1, Pallas kernels, front(): pl.pallas_call(functools.partial(front_kernel, tp_size, cp_size), out_sha...  118 us
    pallas_call x1, Pallas kernels, back(): pl.pallas_call(functools.partial(back_kernel, tp_size, cp_size), out_shap...  117 us

profile of v3, /device:TPU:0, one launch (start us, length us, event | category | flops | bytes accessed | tf_op | source)
XLA Modules:
  0.0 237.6 jit_solution(7869126513917632283)
XLA Ops:
  0.0 117.7 %front.1 = (bf16[2048,256]{1,0:T(8,128)(2,1)}, bf16[16384,256]{1,0:T(8,128)(2,1)}) custom-call(bf16[128,4608]{1,0:T(8,128)(2,1)} %x_hbm.1, bf16[4608,256]{1,0:T(8,128)(2,1)} %wq_hbm.1, bf16[4608,128]{1,0:T(8,128)(2,1)} %wk_hbm.1, bf16[4608,128]{1,0:T(8,128)(2,1)} %wv_hbm.1), custom_call_target="tpu_custom_call" | custom-call | flops 9663676416 | bytes 18874368 | tf_op jit(solution)/shard_map/front/pallas_call | solution.py:164
  117.7 117.5 %back.1 = bf16[128,4608]{1,0:T(8,128)(2,1)} custom-call(bf16[2048,256]{1,0:T(8,128)(2,1)} %get-tuple-element.7.q_hbm, bf16[16384,256]{1,0:T(8,128)(2,1)} %get-tuple-element.8.kv_hbm, bf16[256,4608]{1,0:T(8,128)(2,1)} %wo_hbm.1), custom_call_target="tpu_custom_call" | custom-call | flops 22011707392 | bytes 8388608 | tf_op jit(solution)/shard_map/back/pallas_call | solution.py:469
  235.2 2.4 copy.7

commit v4 on v3

v4 whole, which is shorter than its diff:
```python
import functools

import jax
import jax.numpy as jnp
from jax import lax
from jax.experimental import pallas as pl
from jax.experimental.pallas import tpu as pltpu
from jax.sharding import PartitionSpec as P

HEAD_DIM = 128
LOG2E = 1.4426950408889634
NT = (((1,), (1,)), ((), ()))
SUB = 512


MESH = pl.DeviceIdType.MESH
X_SUB = 2


def layer_kernel(tp_size, cp_size, x_hbm, wq_hbm, wk_hbm, wv_hbm, wo_hbm, y_hbm, xg, w_in, q_buf, kv, w_buf, wo_buf, og, o_buf, y_send, y_all, relay, acc_ref, m_ref, l_ref, load_sem, ring_send, ring_recv, kv_send, left_recv, right_recv, far_recv, pair_recv, w_send, w_recv, d1_send, d1_recv, d2_send, d2_recv, d3_send, d3_recv, relay_recv):
    tp = lax.axis_index("tp")
    cp = lax.axis_index("cp")
    side = 4
    zi, yi = tp // side, lax.rem(tp, side)
    chip, core = cp // 2, lax.rem(cp, 2)
    n_chip = cp_size // 2
    rows = x_hbm.shape[0]
    piece = q_buf.shape[0] // 2
    group = q_buf.shape[1] // HEAD_DIM
    chunk = SUB // side
    slab = wo_buf.shape[0]
    head_rows = slab * cp_size
    cols = w_buf.shape[1]
    coef = LOG2E * HEAD_DIM ** -0.5
    up = lax.rem(zi + 1, side)
    down = lax.rem(zi + side - 1, side)
    z_far = lax.rem(zi + 2, side)
    block = rows * tp_size
    part = rows // 4
    sub = part // X_SUB
    q_width = wq_hbm.shape[1]
    k_width = wk_hbm.shape[1]
    pos = (zi * side + lax.rem(yi + zi, side), yi * side + lax.rem(zi + yi, side))

    def member(cycle, k):
        k = lax.rem(k + 2 * tp_size, tp_size)
        major = k // side
        minor = lax.rem(k - major + side, side)
        return major * side + minor if cycle == 0 else minor * side + major

    streams = [(0, 1), (0, -1), (1, 1), (1, -1)]
    nxt = [member(c, pos[c] + d) for c, d in streams]
    right = lax.rem(chip + 1, n_chip) * 2 + core
    left = lax.rem(chip + n_chip - 1, n_chip) * 2 + core
    far = lax.rem(chip + 2, n_chip) * 2 + core
    pair = cp + 1 - 2 * core
    ahead = jnp.where(core == 0, right, left)
    behind = jnp.where(core == 0, left, right)

    w_q = pltpu.make_async_copy(wq_hbm, w_in.at[:, pl.ds(0, q_width)], load_sem.at[0])
    w_k = pltpu.make_async_copy(wk_hbm, w_in.at[:, pl.ds(q_width, k_width)], load_sem.at[1])
    w_v = pltpu.make_async_copy(wv_hbm, w_in.at[:, pl.ds(q_width + k_width, k_width)], load_sem.at[2])
    own = pltpu.make_async_copy(x_hbm, xg.at[pl.ds(pl.multiple_of(tp * rows, rows), rows)], load_sem.at[3])
    load_w = pltpu.make_async_copy(wo_hbm.at[pl.ds(pl.multiple_of(cp * slab, slab), slab)], wo_buf, load_sem.at[4])
    own.start()
    w_q.start()
    w_k.start()
    w_v.start()
    load_w.start()

    barrier = pltpu.get_barrier_semaphore()
    for k in range(1, tp_size):
        pl.semaphore_signal(barrier, inc=1, device_id={"tp": lax.rem(tp + k, tp_size)}, device_id_type=MESH)
    for peer in (left, right, pair):
        pl.semaphore_signal(barrier, inc=1, device_id={"cp": peer}, device_id_type=MESH)
    pl.semaphore_wait(barrier, tp_size + 2)
    own.wait()

    def source(s, t):
        c, d = streams[s]
        return member(c, pos[c] - d * t)

    def move(src, dst, send_sem, recv_sem, axis, peer):
        return pltpu.make_async_remote_copy(src_ref=src, dst_ref=dst, send_sem=send_sem, recv_sem=recv_sem, device_id={axis: peer}, device_id_type=MESH)

    def kv_rows(owner, s, t):
        return kv.at[pl.ds(pl.multiple_of(owner * block + source(s, t) * rows + s * part, part), part)]

    def got(ref, recv_sem):
        move(ref, ref, w_send.at[0], recv_sem, "cp", pair).wait_recv()

    def sent(ref, send_sem):
        move(ref, ref, send_sem, w_recv.at[0], "cp", pair).wait_send()

    kv_unit = kv.at[pl.ds(0, rows)]

    def kv_own(u):
        for s in range(4):
            at = kv_rows(cp, s, u)
            move(at, at, kv_send.at[0], left_recv.at[u], "cp", right).start()
            move(at, at, kv_send.at[1], right_recv.at[u], "cp", left).start()
            move(at, at, kv_send.at[2], pair_recv.at[0], "cp", pair).start()

    def kv_forward(u):
        got(kv_unit, left_recv.at[u])
        got(kv_unit, right_recv.at[u])
        for s in range(4):
            at = kv_rows(behind, s, u)
            move(at, at, kv_send.at[3], far_recv.at[u], "cp", ahead).start()
            at = kv_rows(left, s, u)
            move(at, at, kv_send.at[4], pair_recv.at[1], "cp", pair).start()
            at = kv_rows(right, s, u)
            move(at, at, kv_send.at[5], pair_recv.at[2], "cp", pair).start()

    def kv_far(u):
        got(kv_unit, far_recv.at[u])
        for s in range(4):
            at = kv_rows(far, s, u)
            move(at, at, kv_send.at[6], pair_recv.at[3], "cp", pair).start()

    def w_rows(owner, member):
        return w_buf.at[pl.ds(pl.multiple_of(owner * head_rows + member * slab, slab), slab)]

    def w_cols(quarter):
        return wo_buf.at[:, pl.ds(pl.multiple_of(quarter * cols, 128), cols)]

    own_w = pltpu.make_async_copy(w_cols(zi), w_rows(tp, cp), load_sem.at[5])

    def spread(k, _):
        peer = lax.rem(tp + k, tp_size)
        move(w_cols(peer // side), w_rows(tp, cp), w_send.at[0], w_recv.at[0], "tp", peer).start()
        return 0

    def step(t, _):
        @pl.when(t == tp_size - 1)
        def _():
            load_w.wait()
            own_w.start()
            lax.fori_loop(1, tp_size, spread, 0)

        for u in range(X_SUB):
            for s in range(4):
                at = xg.at[pl.ds(pl.multiple_of(source(s, t) * rows + s * part + u * sub, sub), sub)]

                @pl.when(t > 0)
                def _():
                    move(at, at, ring_send.at[s], ring_recv.at[s, t - 1, u], "tp", nxt[s]).wait_recv()

                @pl.when(t < tp_size - 1)
                def _():
                    move(at, at, ring_send.at[s], ring_recv.at[s, t, u], "tp", nxt[s]).start()

        @pl.when(t >= 1)
        def _():
            kv_own(t - 1)

        @pl.when(t >= 2)
        def _():
            kv_forward(t - 2)

        @pl.when(t >= 3)
        def _():
            kv_far(t - 3)

        @pl.when(t == 0)
        def _():
            w_q.wait()
            w_k.wait()
            w_v.wait()

        offs = [pl.multiple_of(source(s, t) * rows + s * part, part) for s in range(4)]
        lhs = jnp.concatenate([xg[pl.ds(o, part), :] for o in offs], axis=0)
        res = jnp.dot(lhs, w_in[...], preferred_element_type=jnp.float32).astype(jnp.bfloat16)
        for s in range(4):
            q_buf[pl.ds(offs[s], part), :] = res[s * part:(s + 1) * part, 0:q_width]
            kv[pl.ds(pl.multiple_of(cp * block + offs[s], part), part), :] = res[s * part:(s + 1) * part, q_width:]
        return 0

    lax.fori_loop(0, tp_size, step, 0)
    kv_own(tp_size - 1)
    kv_forward(tp_size - 2)
    kv_far(tp_size - 3)

    def w_share():
        own_w.wait()
        got(w_buf.at[pl.ds(0, (tp_size - 1) * slab)], w_recv.at[0])

        def one(s, _):
            ref = w_rows(s, cp)
            move(ref, ref, w_send.at[1], w_recv.at[1], "cp", right).start()
            move(ref, ref, w_send.at[2], w_recv.at[2], "cp", left).start()
            move(ref, ref, w_send.at[3], w_recv.at[4], "cp", pair).start()
            return 0

        lax.fori_loop(0, tp_size, one, 0)

    w_part = w_buf.at[pl.ds(0, tp_size * slab)]

    def w_pass():
        got(w_part, w_recv.at[1])
        got(w_part, w_recv.at[2])

        def one(s, _):
            ref = w_rows(s, behind)
            move(ref, ref, w_send.at[4], w_recv.at[3], "cp", ahead).start()
            ref = w_rows(s, left)
            move(ref, ref, w_send.at[5], w_recv.at[5], "cp", pair).start()
            ref = w_rows(s, right)
            move(ref, ref, w_send.at[6], w_recv.at[6], "cp", pair).start()
            return 0

        lax.fori_loop(0, tp_size, one, 0)

    def w_last():
        got(w_part, w_recv.at[3])

        def one(s, _):
            ref = w_rows(s, far)
            move(ref, ref, w_send.at[7], w_recv.at[7], "cp", pair).start()
            return 0

        lax.fori_loop(0, tp_size, one, 0)

    def lane_sum(p):
        total = p[:, 0:128]
        for c in range(1, p.shape[1] // 128):
            total = total + p[:, c * 128:(c + 1) * 128]
        return total

    def scores(i, g, base, width):
        qs = q_buf[pl.ds(pl.multiple_of(i * SUB, SUB), SUB), g * HEAD_DIM:(g + 1) * HEAD_DIM]
        ks = kv[pl.ds(pl.multiple_of(base, SUB), width), 0:HEAD_DIM]
        return lax.dot_general(qs, ks, NT, preferred_element_type=jnp.float32)

    def values(p, base, width):
        vs = kv[pl.ds(pl.multiple_of(base, SUB), width), HEAD_DIM:2 * HEAD_DIM]
        return jnp.dot(p.astype(jnp.bfloat16), vs, preferred_element_type=jnp.float32)

    def diag(i, s):
        width = (s + 1) * SUB
        base = cp * 2 * piece + (i // 2) * piece
        for g in range(group):
            sc = scores(i, g, base, width)
            row = lax.broadcasted_iota(jnp.int32, (SUB, width), 0) + s * SUB
            col = lax.broadcasted_iota(jnp.int32, (SUB, width), 1)
            sc = jnp.where(row >= col, sc, -jnp.inf)
            top = jnp.max(sc, axis=1, keepdims=True) * coef
            p = jnp.exp2(sc * coef - top)
            m_ref[g] = jnp.broadcast_to(top, (SUB, 128))
            l_ref[g] = lane_sum(p)
            acc_ref[g] = values(p, base, width)

    def d1(i, k):
        peer = lax.rem(yi + k, side)
        return move(o_buf.at[i, peer], og.at[i, tp], d1_send.at[0], d1_recv.at[i], "tp", zi * side + peer)

    def tile_part(i, z, half):
        return og.at[i, pl.ds(z * side, side), pl.ds(half * (chunk // 2), chunk // 2)]

    def d2(i, z, half, send, recv, peer):
        ref = tile_part(i, z, half)
        return move(ref, ref, d2_send.at[send], d2_recv.at[i, recv], "tp", peer * side + yi)

    def gather_start(i):
        got(og.at[i, pl.ds(0, side - 1)], d1_recv.at[i])
        d2(i, zi, 0, 0, 0, up).start()
        d2(i, zi, 1, 1, 2, down).start()
        d2(i, zi, 1, 0, 1, up).start()
        d2(i, zi, 0, 1, 3, down).start()

    def gather_pass(i):
        got(tile_part(i, down, 0), d2_recv.at[i, 0])
        d2(i, down, 0, 2, 4, up).start()
        got(tile_part(i, up, 1), d2_recv.at[i, 2])
        d2(i, up, 1, 3, 5, down).start()

    def gather_end(i):
        got(tile_part(i, down, 1), d2_recv.at[i, 1])
        got(tile_part(i, up, 0), d2_recv.at[i, 3])
        got(tile_part(i, z_far, 0), d2_recv.at[i, 4])
        got(tile_part(i, z_far, 1), d2_recv.at[i, 5])

    y_mine = y_all.at[:, pl.ds(pl.multiple_of(zi * cols, 128), cols)]

    def project(i):
        lhs = jnp.concatenate([og[i, s] for s in range(tp_size)], axis=1)
        y_send[i] = jnp.dot(lhs, w_buf[...], preferred_element_type=jnp.float32).astype(jnp.bfloat16)

    half = chunk // 2

    def y_part(h, z):
        return y_all.at[pl.ds(h * half, half), pl.ds(pl.multiple_of(z * cols, 128), cols)]

    def deliver(i):
        dist = lax.rem(i - zi + side, side)

        @pl.when(lax.rem(dist, 2) == 1)
        def _():
            move(y_send.at[i], y_mine, d3_send.at[0], d3_recv.at[0], "tp", i * side + yi).start()

        @pl.when(dist == 2)
        def _():
            move(y_send.at[i, pl.ds(0, half)], relay.at[0], d3_send.at[1], relay_recv.at[0], "tp", up * side + yi).start()
            move(y_send.at[i, pl.ds(half, half)], relay.at[1], d3_send.at[1], relay_recv.at[1], "tp", down * side + yi).start()

        @pl.when(dist == 0)
        def _():
            y_all[:, pl.ds(pl.multiple_of(zi * cols, 128), cols)] = y_send[i]

    def hand_on(i):
        dist = lax.rem(i - zi + side, side)

        @pl.when(dist == 1)
        def _():
            got(relay.at[0], relay_recv.at[0])
            move(relay.at[0], y_part(0, down), d3_send.at[2], d3_recv.at[1], "tp", up * side + yi).start()

        @pl.when(dist == 3)
        def _():
            got(relay.at[1], relay_recv.at[1])
            move(relay.at[1], y_part(1, up), d3_send.at[3], d3_recv.at[2], "tp", down * side + yi).start()

    def tile(i, _):
        is_low = i < 2
        count = jnp.where(is_low, cp, 2 * cp_size - 1 - cp)
        before = jnp.where(is_low, i * cp, 2 * cp + (i - 2) * (2 * cp_size - 1 - cp))

        @pl.when(lax.rem(i, 2) == 0)
        def _():
            diag(i, 0)

        @pl.when(lax.rem(i, 2) == 1)
        def _():
            diag(i, 1)

        @pl.when(i == 0)
        def _():
            kv_forward(tp_size - 1)
            kv_far(tp_size - 2)
            kv_far(tp_size - 1)
            for k in range(4):
                got(kv.at[pl.ds(0, block)], pair_recv.at[k])

        @pl.when(i == 2)
        def _():
            gather_start(0)
            gather_start(1)

        @pl.when(i == 3)
        def _():
            gather_start(2)

        def full(j, _):
            first = j < cp_size
            base = jnp.where(first, j * 2 * piece, (2 * cp_size - 1 - j) * 2 * piece + piece)
            turn = before + j
            pl.when(turn == 6)(w_share)
            pl.when(turn == 21)(w_pass)
            pl.when(turn == 28)(w_last)
            nxt = scores(i, 0, base, piece)
            for g in range(group):
                sc = nxt
                if g + 1 < group:
                    nxt = scores(i, g + 1, base, piece)
                m_old = m_ref[g]
                top = jnp.max(sc, axis=1, keepdims=True) * coef
                m_new = jnp.maximum(m_old, top)
                scale = jnp.exp2(m_old - m_new)
                p = jnp.exp2(sc * coef - m_new[:, 0:1])
                m_ref[g] = m_new
                l_ref[g] = l_ref[g] * scale + lane_sum(p)
                acc_ref[g] = acc_ref[g] * scale + values(p, base, piece)
            return 0

        early = jnp.minimum(count, 6)
        lax.fori_loop(0, early, full, 0)

        @pl.when(i == 2)
        def _():
            gather_pass(0)
            gather_pass(1)

        @pl.when(i == 3)
        def _():
            gather_pass(2)

        lax.fori_loop(early, count, full, 0)
        for g in range(group):
            total = jnp.sum(l_ref[g], axis=1, keepdims=True)
            out = (acc_ref[g] / total).astype(jnp.bfloat16)
            for k in range(side):
                o_buf[i, k, :, g * HEAD_DIM:(g + 1) * HEAD_DIM] = out[k * chunk:(k + 1) * chunk]
        og[i, tp] = o_buf[i, yi]
        for k in range(1, side):
            d1(i, k).start()
        return 0

    lax.fori_loop(0, side, tile, 0)

    gather_start(3)
    for k in range(4, 8):
        got(w_part, w_recv.at[k])
    for i in range(3):
        gather_end(i)
    lax.fori_loop(0, 3, lambda i, c: (project(i), c)[1], 0)
    gather_pass(3)
    for i in range(3):
        deliver(i)
    gather_end(3)
    project(3)
    deliver(3)
    for i in range(4):
        hand_on(i)
    got(y_all.at[:, pl.ds(0, 2 * cols)], d3_recv.at[0])
    got(relay.at[0], d3_recv.at[1])
    got(relay.at[1], d3_recv.at[2])
    out = pltpu.make_async_copy(y_all, y_hbm, load_sem.at[0])
    out.start()
    for s in range(4):
        sent(xg.at[pl.ds(0, (tp_size - 1) * part)], ring_send.at[s])
    for k in range(7):
        sent(kv.at[pl.ds(0, block)], kv_send.at[k])
    sent(w_buf.at[pl.ds(0, (tp_size - 1) * slab)], w_send.at[0])
    for k in range(1, 8):
        sent(w_part, w_send.at[k])
    sent(o_buf.at[:, pl.ds(0, side - 1)], d1_send.at[0])
    sent(og.at[:, pl.ds(0, side)], d2_send.at[0])
    sent(og.at[:, pl.ds(0, side)], d2_send.at[1])
    sent(og.at[:, pl.ds(0, side), pl.ds(0, chunk // 2)], d2_send.at[2])
    sent(og.at[:, pl.ds(0, side), pl.ds(0, chunk // 2)], d2_send.at[3])
    sent(y_send.at[pl.ds(0, 2)], d3_send.at[0])
    sent(y_send.at[0], d3_send.at[1])
    sent(relay.at[0], d3_send.at[2])
    sent(relay.at[1], d3_send.at[3])
    out.wait()


def layer(tp_size, cp_size, x_loc, w_q, w_k, w_v, w_o):
    rows, depth = x_loc.shape
    block = rows * tp_size
    q_width = w_q.shape[1]
    kv_width = w_k.shape[1] + w_v.shape[1]
    group = q_width // HEAD_DIM
    model_width = w_o.shape[1]
    side = 4
    cols = model_width // side
    any_space = pl.BlockSpec(memory_space=pl.ANY)
    dma = pltpu.SemaphoreType.DMA
    bf16 = jnp.bfloat16
    flops = 2 * block * depth * (2 * q_width + kv_width) + 2 * block * q_width * block * cp_size
    return pl.pallas_call(
        functools.partial(layer_kernel, tp_size, cp_size),
        out_shape=jax.ShapeDtypeStruct((rows, model_width), bf16),
        in_specs=[any_space] * 5,
        out_specs=any_space,
        scratch_shapes=[
            pltpu.VMEM((block, depth), bf16),
            pltpu.VMEM((depth, q_width + kv_width), bf16),
            pltpu.VMEM((block, q_width), bf16),
            pltpu.VMEM((block * cp_size, kv_width), bf16),
            pltpu.VMEM((w_o.shape[0] * tp_size, cols), bf16),
            pltpu.VMEM((w_o.shape[0] // cp_size, model_width), bf16),
            pltpu.VMEM((side, tp_size, rows, q_width), bf16),
            pltpu.VMEM((side, side, rows, q_width), bf16),
            pltpu.VMEM((side, rows, cols), bf16),
            pltpu.VMEM((rows, model_width), bf16),
            pltpu.VMEM((2, rows // 2, cols), bf16),
        ] + [pltpu.VMEM((group, SUB, 128), jnp.float32) for _ in range(3)] + [
            dma((6,)), dma((4,)), dma((4, tp_size - 1, X_SUB)), dma((7,)), dma((tp_size,)), dma((tp_size,)), dma((tp_size,)), dma((4,)),
            dma((8,)), dma((8,)), dma((1,)), dma((side,)), dma((4,)), dma((side, 6)), dma((4,)), dma((3,)), dma((2,)),
        ],
        compiler_params=pltpu.CompilerParams(collective_id=0, has_side_effects=True, vmem_limit_bytes=67043328),
        cost_estimate=pl.CostEstimate(flops=flops, bytes_accessed=block * depth * 2, transcendentals=0),
        name="layer",
    )(x_loc, w_q, w_k, w_v, w_o)


def solution(mesh):
    cp_size = mesh.shape["cp"]
    tp_size = mesh.shape["tp"]
    row_spec = P(("dp", "cp", "tp"), None)
    local_layer = functools.partial(layer, tp_size, cp_size)
    return jax.shard_map(local_layer, mesh=mesh, in_specs=(row_spec, P(None, "tp"), P(None, "tp"), P(None, "tp"), P("tp", None)), out_specs=row_spec, check_vma=False)
```

time: 239 us -> 224 us (0.937)
  Pallas kernels: 235 us -> 221 us
    pallas_call x2 -> x1, Pallas kernels: 235 us -> 221 us  [layer(): pl.pallas_call(functools.partial(layer_kernel, tp_size, cp_size), out_sha...]
where the time goes in v4:
time: 224 us; the launch traced here: 223 us
  Pallas kernels  221 us (99%)
  local copies, waits for them, and re-layouts  2.36 us (1%)
    pallas_call x1, Pallas kernels, layer(): pl.pallas_call(functools.partial(layer_kernel, tp_size, cp_size), out_sha...  221 us

profile of v4, /device:TPU:0, one launch (start us, length us, event | category | flops | bytes accessed | tf_op | source)
XLA Modules:
  0.0 223.0 jit_solution(2742850549519534349)
XLA Ops:
  0.0 220.6 %layer.1 = bf16[128,4608]{1,0:T(8,128)(2,1)} custom-call(bf16[128,4608]{1,0:T(8,128)(2,1)} %x_hbm.1, bf16[4608,256]{1,0:T(8,128)(2,1)} %wq_hbm.1, bf16[4608,128]{1,0:T(8,128)(2,1)} %wk_hbm.1, bf16[4608,128]{1,0:T(8,128)(2,1)} %wv_hbm.1, bf16[256,4608]{1,0:T(8,128)(2,1)} %wo_hbm.1), custom_call_target="tpu_custom_call" | custom-call | flops 31675383808 | bytes 18874368 | tf_op jit(solution)/shard_map/layer/pallas_call | solution.py:451
  220.6 2.4 %copy.7 = bf16[128,4608]{1,0:T(8,128)(2,1)} copy(bf16[128,4608]{1,0:T(8,128)(2,1)} %layer.1) | data formatting | bytes 2359296

commit v5 on v4

--- a/solution.py
+++ b/solution.py
@@ -17,7 +17,7 @@
 X_SUB = 2
 
 
-def layer_kernel(tp_size, cp_size, x_hbm, wq_hbm, wk_hbm, wv_hbm, wo_hbm, y_hbm, xg, w_in, q_buf, kv, w_buf, wo_buf, og, o_buf, y_send, y_all, relay, acc_ref, m_ref, l_ref, load_sem, ring_send, ring_recv, kv_send, left_recv, right_recv, far_recv, pair_recv, w_send, w_recv, d1_send, d1_recv, d2_send, d2_recv, d3_send, d3_recv, relay_recv):
+def layer_kernel(tp_size, cp_size, x_hbm, wq_hbm, wk_hbm, wv_hbm, wo_hbm, y_hbm, xg, w_in, q_buf, kv, w_buf, wo_buf, og, o_buf, y_send, y_all, relay, acc_ref, m_ref, l_ref, x_ref, s_even, s_odd, load_sem, ring_send, ring_recv, kv_send, left_recv, right_recv, far_recv, pair_recv, w_send, w_recv, d1_send, d1_recv, d2_send, d2_recv, d3_send, d3_recv, relay_recv):
     tp = lax.axis_index("tp")
     cp = lax.axis_index("cp")
     side = 4
@@ -126,17 +126,25 @@
 
     own_w = pltpu.make_async_copy(w_cols(zi), w_rows(tp, cp), load_sem.at[5])
 
-    def spread(k, _):
-        peer = lax.rem(tp + k, tp_size)
-        move(w_cols(peer // side), w_rows(tp, cp), w_send.at[0], w_recv.at[0], "tp", peer).start()
-        return 0
+    n_group = 4
+    per_group = tp_size // n_group
+
+    def w_fetch():
+        for k in range(1, tp_size):
+            peer = lax.rem(tp + k, tp_size)
+            move(w_cols(peer // side), w_rows(tp, cp), w_send.at[0], w_recv.at[k // per_group], "tp", peer).start()
+
+    def w_sources(grp):
+        return [lax.rem(tp - k + tp_size, tp_size) for k in range(grp * per_group, (grp + 1) * per_group)]
+
+    w_group = w_buf.at[pl.ds(0, per_group * slab)]
 
     def step(t, _):
         @pl.when(t == tp_size - 1)
         def _():
             load_w.wait()
             own_w.start()
-            lax.fori_loop(1, tp_size, spread, 0)
+            w_fetch()
 
         for u in range(X_SUB):
             for s in range(4):
@@ -181,74 +189,65 @@
     kv_forward(tp_size - 2)
     kv_far(tp_size - 3)
 
-    def w_share():
-        own_w.wait()
-        got(w_buf.at[pl.ds(0, (tp_size - 1) * slab)], w_recv.at[0])
-
-        def one(s, _):
-            ref = w_rows(s, cp)
-            move(ref, ref, w_send.at[1], w_recv.at[1], "cp", right).start()
-            move(ref, ref, w_send.at[2], w_recv.at[2], "cp", left).start()
-            move(ref, ref, w_send.at[3], w_recv.at[4], "cp", pair).start()
-            return 0
-
-        lax.fori_loop(0, tp_size, one, 0)
+    def w_share(grp):
+        if grp == 0:
+            own_w.wait()
+            got(w_buf.at[pl.ds(0, (per_group - 1) * slab)], w_recv.at[0])
+        else:
+            got(w_group, w_recv.at[grp])
+        for o in w_sources(grp):
+            ref = w_rows(o, cp)
+            move(ref, ref, w_send.at[1], w_recv.at[4 + grp], "cp", right).start()
+            move(ref, ref, w_send.at[2], w_recv.at[8 + grp], "cp", left).start()
+            move(ref, ref, w_send.at[3], w_recv.at[16], "cp", pair).start()
+
+    def w_pass(grp):
+        got(w_group, w_recv.at[4 + grp])
+        got(w_group, w_recv.at[8 + grp])
+        for o in w_sources(grp):
+            ref = w_rows(o, behind)
+            move(ref, ref, w_send.at[4], w_recv.at[12 + grp], "cp", ahead).start()
+            ref = w_rows(o, left)
+            move(ref, ref, w_send.at[5], w_recv.at[17], "cp", pair).start()
+            ref = w_rows(o, right)
+            move(ref, ref, w_send.at[6], w_recv.at[18], "cp", pair).start()
+
+    def w_last(grp):
+        got(w_group, w_recv.at[12 + grp])
+        for o in w_sources(grp):
+            ref = w_rows(o, far)
+            move(ref, ref, w_send.at[7], w_recv.at[19], "cp", pair).start()
 
     w_part = w_buf.at[pl.ds(0, tp_size * slab)]
 
-    def w_pass():
-        got(w_part, w_recv.at[1])
-        got(w_part, w_recv.at[2])
-
-        def one(s, _):
-            ref = w_rows(s, behind)
-            move(ref, ref, w_send.at[4], w_recv.at[3], "cp", ahead).start()
-            ref = w_rows(s, left)
-            move(ref, ref, w_send.at[5], w_recv.at[5], "cp", pair).start()
-            ref = w_rows(s, right)
-            move(ref, ref, w_send.at[6], w_recv.at[6], "cp", pair).start()
-            return 0
-
-        lax.fori_loop(0, tp_size, one, 0)
-
-    def w_last():
-        got(w_part, w_recv.at[3])
-
-        def one(s, _):
-            ref = w_rows(s, far)
-            move(ref, ref, w_send.at[7], w_recv.at[7], "cp", pair).start()
-            return 0
-
-        lax.fori_loop(0, tp_size, one, 0)
-
-    def lane_sum(p):
-        total = p[:, 0:128]
-        for c in range(1, p.shape[1] // 128):
-            total = total + p[:, c * 128:(c + 1) * 128]
+    def fold(x, op):
+        total = x[0:8]
+        for c in range(1, x.shape[0] // 8):
+            total = op(total, x[c * 8:(c + 1) * 8])
         return total
 
     def scores(i, g, base, width):
         qs = q_buf[pl.ds(pl.multiple_of(i * SUB, SUB), SUB), g * HEAD_DIM:(g + 1) * HEAD_DIM]
         ks = kv[pl.ds(pl.multiple_of(base, SUB), width), 0:HEAD_DIM]
-        return lax.dot_general(qs, ks, NT, preferred_element_type=jnp.float32)
+        return lax.dot_general(ks, qs, NT, preferred_element_type=jnp.float32)
 
     def values(p, base, width):
         vs = kv[pl.ds(pl.multiple_of(base, SUB), width), HEAD_DIM:2 * HEAD_DIM]
-        return jnp.dot(p.astype(jnp.bfloat16), vs, preferred_element_type=jnp.float32)
+        return jnp.dot(vs.T, p, preferred_element_type=jnp.float32)
 
     def diag(i, s):
         width = (s + 1) * SUB
         base = cp * 2 * piece + (i // 2) * piece
         for g in range(group):
             sc = scores(i, g, base, width)
-            row = lax.broadcasted_iota(jnp.int32, (SUB, width), 0) + s * SUB
-            col = lax.broadcasted_iota(jnp.int32, (SUB, width), 1)
-            sc = jnp.where(row >= col, sc, -jnp.inf)
-            top = jnp.max(sc, axis=1, keepdims=True) * coef
+            key = lax.broadcasted_iota(jnp.int32, (width, SUB), 0)
+            query = lax.broadcasted_iota(jnp.int32, (width, SUB), 1) + s * SUB
+            sc = jnp.where(query >= key, sc, -jnp.inf)
+            top = jnp.max(sc, axis=0, keepdims=True) * coef
             p = jnp.exp2(sc * coef - top)
-            m_ref[g] = jnp.broadcast_to(top, (SUB, 128))
-            l_ref[g] = lane_sum(p)
-            acc_ref[g] = values(p, base, width)
+            m_ref[g, 0:1, :] = top
+            l_ref[g] = fold(p, jnp.add)
+            acc_ref[g] = values(p.astype(jnp.bfloat16), base, width)
 
     def d1(i, k):
         peer = lax.rem(yi + k, side)
@@ -341,53 +340,68 @@
             for k in range(4):
                 got(kv.at[pl.ds(0, block)], pair_recv.at[k])
 
-        @pl.when(i == 2)
-        def _():
-            gather_start(0)
-            gather_start(1)
-
-        @pl.when(i == 3)
-        def _():
-            gather_start(2)
+        def piece_base(j):
+            return jnp.where(j < cp_size, j * 2 * piece, (2 * cp_size - 1 - j) * 2 * piece + piece)
+
+        def look(g, base):
+            ahead_sc = scores(i, g, base, piece)
+            s_ref[g][...] = ahead_sc
+            return ahead_sc
 
         def full(j, _):
-            first = j < cp_size
-            base = jnp.where(first, j * 2 * piece, (2 * cp_size - 1 - j) * 2 * piece + piece)
+            base = piece_base(j)
+            later = piece_base(jnp.minimum(j + 1, count - 1))
             turn = before + j
-            pl.when(turn == 6)(w_share)
-            pl.when(turn == 21)(w_pass)
-            pl.when(turn == 28)(w_last)
-            nxt = scores(i, 0, base, piece)
+            for grp, at in enumerate((0, 1, 3, 7)):
+                pl.when(turn == at)(functools.partial(w_share, grp))
+            for grp, at in enumerate((9, 14, 19, 24)):
+                pl.when(turn == at)(functools.partial(w_pass, grp))
+            for grp, at in enumerate((27, 29)):
+                pl.when(turn == at)(functools.partial(w_last, grp))
+
+            @pl.when(turn == low_turn)
+            def _():
+                gather_start(0)
+                gather_start(1)
+
+            @pl.when(turn == low_turn + 9)
+            def _():
+                gather_pass(0)
+                gather_pass(1)
+
+            @pl.when(turn == cp + 2 * cp_size + 2)
+            def _():
+                gather_start(2)
+
+            @pl.when(turn == cp + 2 * cp_size + 6)
+            def _():
+                gather_pass(2)
+
             for g in range(group):
-                sc = nxt
-                if g + 1 < group:
-                    nxt = scores(i, g + 1, base, piece)
-                m_old = m_ref[g]
-                top = jnp.max(sc, axis=1, keepdims=True) * coef
+                top = jnp.max(x_ref[g], axis=0, keepdims=True) * coef
+                m_old = m_ref[g, 0:1, :]
                 m_new = jnp.maximum(m_old, top)
                 scale = jnp.exp2(m_old - m_new)
-                p = jnp.exp2(sc * coef - m_new[:, 0:1])
-                m_ref[g] = m_new
-                l_ref[g] = l_ref[g] * scale + lane_sum(p)
+                m_ref[g, 0:1, :] = m_new
+                total = l_ref[g] * scale
+                nxt = look((g + 1) % group, base if g + 1 < group else later)
+                p = jnp.exp2(s_ref[g][...] * coef - m_new)
+                total = total + fold(p, jnp.add)
+                p = p.astype(jnp.bfloat16)
+                peak = fold(nxt, jnp.maximum)
                 acc_ref[g] = acc_ref[g] * scale + values(p, base, piece)
+                l_ref[g] = total
+                x_ref[(g + 1) % group] = peak
             return 0
 
-        early = jnp.minimum(count, 6)
-        lax.fori_loop(0, early, full, 0)
-
-        @pl.when(i == 2)
-        def _():
-            gather_pass(0)
-            gather_pass(1)
-
-        @pl.when(i == 3)
-        def _():
-            gather_pass(2)
-
-        lax.fori_loop(early, count, full, 0)
+        @pl.when(count > 0)
+        def _():
+            x_ref[0] = fold(look(0, piece_base(0)), jnp.maximum)
+
+        lax.fori_loop(0, count, full, 0)
         for g in range(group):
-            total = jnp.sum(l_ref[g], axis=1, keepdims=True)
-            out = (acc_ref[g] / total).astype(jnp.bfloat16)
+            total = jnp.sum(l_ref[g], axis=0, keepdims=True)
+            out = (acc_ref[g] / total).T.astype(jnp.bfloat16)
             for k in range(side):
                 o_buf[i, k, :, g * HEAD_DIM:(g + 1) * HEAD_DIM] = out[k * chunk:(k + 1) * chunk]
         og[i, tp] = o_buf[i, yi]
@@ -395,15 +409,20 @@
             d1(i, k).start()
         return 0
 
+    low_turn = jnp.maximum(2 * cp + 2, 12)
+    s_ref = (s_even, s_odd)
     lax.fori_loop(0, side, tile, 0)
 
     gather_start(3)
-    for k in range(4, 8):
+    w_last(2)
+    w_last(3)
+    for k in range(16, 20):
         got(w_part, w_recv.at[k])
     for i in range(3):
         gather_end(i)
-    lax.fori_loop(0, 3, lambda i, c: (project(i), c)[1], 0)
+    project(0)
     gather_pass(3)
+    lax.fori_loop(1, 3, lambda i, c: (project(i), c)[1], 0)
     for i in range(3):
         deliver(i)
     gather_end(3)
@@ -465,9 +484,9 @@
             pltpu.VMEM((side, rows, cols), bf16),
             pltpu.VMEM((rows, model_width), bf16),
             pltpu.VMEM((2, rows // 2, cols), bf16),
-        ] + [pltpu.VMEM((group, SUB, 128), jnp.float32) for _ in range(3)] + [
+        ] + [pltpu.VMEM((group, HEAD_DIM, SUB), jnp.float32)] + [pltpu.VMEM((group, 8, SUB), jnp.float32) for _ in range(3)] + [pltpu.VMEM((block // 2, SUB), jnp.float32) for _ in range(2)] + [
             dma((6,)), dma((4,)), dma((4, tp_size - 1, X_SUB)), dma((7,)), dma((tp_size,)), dma((tp_size,)), dma((tp_size,)), dma((4,)),
-            dma((8,)), dma((8,)), dma((1,)), dma((side,)), dma((4,)), dma((side, 6)), dma((4,)), dma((3,)), dma((2,)),
+            dma((8,)), dma((20,)), dma((1,)), dma((side,)), dma((4,)), dma((side, 6)), dma((4,)), dma((3,)), dma((2,)),
         ],
         compiler_params=pltpu.CompilerParams(collective_id=0, has_side_effects=True, vmem_limit_bytes=67043328),
         cost_estimate=pl.CostEstimate(flops=flops, bytes_accessed=block * depth * 2, transcendentals=0),

time: 224 us -> 215 us (0.960)
  the two profiles are of different devices: /device:TPU:0 before, /device:TPU:50 now
where the time goes in v5:
time: 215 us
  Pallas kernels  212 us (99%)
  local copies, waits for them, and re-layouts  2.36 us (1%)
    pallas_call x1, Pallas kernels, layer(): pl.pallas_call(functools.partial(layer_kernel, tp_size, cp_size), out_sha...  212 us

profile of v5, /device:TPU:50, one launch (start us, length us, event | category | flops | bytes accessed | tf_op | source)
XLA Modules:
  0.0 214.6 jit_solution(8628800051096828852)
XLA Ops:
  0.0 212.2 %layer.1 = bf16[128,4608]{1,0:T(8,128)(2,1)} custom-call(bf16[128,4608]{1,0:T(8,128)(2,1)} %x_hbm.1, bf16[4608,256]{1,0:T(8,128)(2,1)} %wq_hbm.1, bf16[4608,128]{1,0:T(8,128)(2,1)} %wk_hbm.1, bf16[4608,128]{1,0:T(8,128)(2,1)} %wv_hbm.1, bf16[256,4608]{1,0:T(8,128)(2,1)} %wo_hbm.1), custom_call_target="tpu_custom_call" | custom-call | flops 31675383808 | bytes 18874368 | tf_op jit(solution)/shard_map/layer/pallas_call | solution.py:470
  212.2 2.4 %copy.7 = bf16[128,4608]{1,0:T(8,128)(2,1)} copy(bf16[128,4608]{1,0:T(8,128)(2,1)} %layer.1) | data formatting | bytes 2359296

commit v6 on v5

--- a/solution.py
+++ b/solution.py
@@ -352,30 +352,19 @@
             base = piece_base(j)
             later = piece_base(jnp.minimum(j + 1, count - 1))
             turn = before + j
-            for grp, at in enumerate((0, 1, 3, 7)):
-                pl.when(turn == at)(functools.partial(w_share, grp))
-            for grp, at in enumerate((9, 14, 19, 24)):
-                pl.when(turn == at)(functools.partial(w_pass, grp))
-            for grp, at in enumerate((27, 29)):
-                pl.when(turn == at)(functools.partial(w_last, grp))
-
-            @pl.when(turn == low_turn)
-            def _():
-                gather_start(0)
-                gather_start(1)
-
-            @pl.when(turn == low_turn + 9)
-            def _():
-                gather_pass(0)
-                gather_pass(1)
-
-            @pl.when(turn == cp + 2 * cp_size + 2)
-            def _():
-                gather_start(2)
-
-            @pl.when(turn == cp + 2 * cp_size + 6)
-            def _():
-                gather_pass(2)
+            services = [(at, functools.partial(w_share, grp)) for grp, at in enumerate((0, 1, 3, 7))]
+            services += [(at, functools.partial(w_pass, grp)) for grp, at in enumerate((9, 14, 19, 24))]
+            services += [(at, functools.partial(w_last, grp)) for grp, at in enumerate((27, 29))]
+            services += [(low_turn, start_low), (low_turn + 9, pass_low)]
+            services += [(high_turn, functools.partial(gather_start, 2)), (high_turn + 4, functools.partial(gather_pass, 2))]
+            due = functools.reduce(jnp.add, [jnp.where(turn == at, 1, 0) for at, _ in services])
+
+            def serve(_, carry):
+                for at, act in services:
+                    pl.when(turn == at)(act)
+                return carry
+
+            lax.fori_loop(0, jnp.minimum(due, 1), serve, 0)
 
             for g in range(group):
                 top = jnp.max(x_ref[g], axis=0, keepdims=True) * coef
@@ -409,7 +398,16 @@
             d1(i, k).start()
         return 0
 
+    def start_low():
+        gather_start(0)
+        gather_start(1)
+
+    def pass_low():
+        gather_pass(0)
+        gather_pass(1)
+
     low_turn = jnp.maximum(2 * cp + 2, 12)
+    high_turn = cp + 2 * cp_size + 2
     s_ref = (s_even, s_odd)
     lax.fori_loop(0, side, tile, 0)
 

time: 215 us -> 211 us (0.981)
  the two profiles are of different devices: /device:TPU:50 before, /device:TPU:0 now
where the time goes in v6:
time: 211 us; the launch traced here: 207 us
  Pallas kernels  205 us (97%)
  local copies, waits for them, and re-layouts  2.36 us (1%)
    pallas_call x1, Pallas kernels, layer(): pl.pallas_call(functools.partial(layer_kernel, tp_size, cp_size), out_sha...  205 us

profile of v6, /device:TPU:0, one launch (start us, length us, event | category | flops | bytes accessed | tf_op | source)
XLA Modules:
  0.0 207.0 jit_solution(2774871091532325402)
XLA Ops:
  0.0 204.7 %layer.1 = bf16[128,4608]{1,0:T(8,128)(2,1)} custom-call(bf16[128,4608]{1,0:T(8,128)(2,1)} %x_hbm.1, bf16[4608,256]{1,0:T(8,128)(2,1)} %wq_hbm.1, bf16[4608,128]{1,0:T(8,128)(2,1)} %wk_hbm.1, bf16[4608,128]{1,0:T(8,128)(2,1)} %wv_hbm.1, bf16[256,4608]{1,0:T(8,128)(2,1)} %wo_hbm.1), custom_call_target="tpu_custom_call" | custom-call | flops 31675383808 | bytes 18874368 | tf_op jit(solution)/shard_map/layer/pallas_call | solution.py:468
  204.7 2.4 %copy.7 = bf16[128,4608]{1,0:T(8,128)(2,1)} copy(bf16[128,4608]{1,0:T(8,128)(2,1)} %layer.1) | data formatting | bytes 2359296

commit v7 on v6

--- a/solution.py
+++ b/solution.py
@@ -352,10 +352,10 @@
             base = piece_base(j)
             later = piece_base(jnp.minimum(j + 1, count - 1))
             turn = before + j
-            services = [(at, functools.partial(w_share, grp)) for grp, at in enumerate((0, 1, 3, 7))]
-            services += [(at, functools.partial(w_pass, grp)) for grp, at in enumerate((9, 14, 19, 24))]
+            services = [(at, functools.partial(w_share, grp)) for grp, at in enumerate((0, 2, 5, 10))]
+            services += [(at, functools.partial(w_pass, grp)) for grp, at in enumerate((11, 17, 23, 28))]
             services += [(at, functools.partial(w_last, grp)) for grp, at in enumerate((27, 29))]
-            services += [(low_turn, start_low), (low_turn + 9, pass_low)]
+            services += [(low_turn, start_low), (low_turn + 11, pass_low)]
             services += [(high_turn, functools.partial(gather_start, 2)), (high_turn + 4, functools.partial(gather_pass, 2))]
             due = functools.reduce(jnp.add, [jnp.where(turn == at, 1, 0) for at, _ in services])
 

time: 211 us -> 209 us (level)
  no operation moved by 1% of the time
where the time goes in v7:
time: 209 us; the launch traced here: 206 us
  Pallas kernels  204 us (98%)
  local copies, waits for them, and re-layouts  2.36 us (1%)
    pallas_call x1, Pallas kernels, layer(): pl.pallas_call(functools.partial(layer_kernel, tp_size, cp_size), out_sha...  204 us

profile of v7, /device:TPU:0, one launch (start us, length us, event | category | flops | bytes accessed | tf_op | source)
XLA Modules:
  0.0 206.4 jit_solution(1663441302044813495)
XLA Ops:
  0.0 204.1 %layer.1 = bf16[128,4608]{1,0:T(8,128)(2,1)} custom-call(bf16[128,4608]{1,0:T(8,128)(2,1)} %x_hbm.1, bf16[4608,256]{1,0:T(8,128)(2,1)} %wq_hbm.1, bf16[4608,128]{1,0:T(8,128)(2,1)} %wk_hbm.1, bf16[4608,128]{1,0:T(8,128)(2,1)} %wv_hbm.1, bf16[256,4608]{1,0:T(8,128)(2,1)} %wo_hbm.1), custom_call_target="tpu_custom_call" | custom-call | flops 31675383808 | bytes 18874368 | tf_op jit(solution)/shard_map/layer/pallas_call | solution.py:468
  204.1 2.4 %copy.7 = bf16[128,4608]{1,0:T(8,128)(2,1)} copy(bf16[128,4608]{1,0:T(8,128)(2,1)} %layer.1) | data formatting | bytes 2359296
